TPU v7x, 32 devices: a whole 2x2x4 slice. The times are simulated.
32 devices in a mesh: rows: 4 (over y, x), feat: 8 (over z, core).
Axes of the slice: x: 2, y: 2, z: 4, core: 2. Of those that a mesh axis runs over, the one named last changes fastest.
Arguments:
- bins: int32 [768, 16384], P('feat', 'rows'), may hold values from 0 to 255
- fold: int32 [16384], P('rows'), may hold values from 0 to 9
- nodes: int32 [16384, 10], P('rows'), may hold values from 0 to 3
- gradient: bfloat16 [16384], P('rows'), may hold values from -6 to 6
- hessian: bfloat16 [16384], P('rows'), may hold values from 0.049804688 to 1
Outputs:
- train_hist: float32 [80, 768, 256], P('rows', 'feat')
- node_gain: float32 [10, 4], replicated
All inputs are finite; a program needn't handle non-finite values.
Results may differ from a plain program's by a relative error of at most 0.0003.
Values sent between devices are 32-bit elements; how exact they have to be, the bound alone decides.
No kernel may reach another device: no remote copies, remote signals or barrier semaphores. Data moves between devices by JAX's collectives and lax.ppermute only.
A program may use at most 64 MiB of HBM per device.

v0:
```python
import jax
import jax.numpy as jnp
from jax import lax
from jax.sharding import PartitionSpec as P

BINS = 256
FOLDS = 10
NODES = 4


def accumulate(bins, weights):
    feats, rows_here = bins.shape
    block = min(512, rows_here)
    group = min(16, feats)
    columns = weights.shape[0]
    levels = jnp.arange(BINS, dtype=jnp.int32)[:, None]

    def visit(turn, total):
        start = turn * block
        part_bins = lax.dynamic_slice_in_dim(bins, start, block, 1)
        part_weights = lax.dynamic_slice_in_dim(weights, start, block, 1)
        for first in range(0, feats, group):
            onehot = (part_bins[first : first + group, None, :] == levels[None]).astype(
                jnp.bfloat16
            )
            term = jnp.einsum(
                "cr,fbr->cfb", part_weights, onehot, preferred_element_type=jnp.float32
            )
            total = total.at[:, first : first + group].add(term)
        return total

    empty = jnp.zeros((columns, feats, BINS), jnp.float32)
    return lax.fori_loop(0, rows_here // block, visit, empty)


def on_device(bins, fold, nodes, gradient, hessian):
    feats, rows_here = bins.shape
    grad = gradient.astype(jnp.float32)[:, None]
    hess = hessian.astype(jnp.float32)[:, None]
    kept = (fold[:, None] != jnp.arange(FOLDS, dtype=jnp.int32)[None, :])[:, :, None]
    node_hot = nodes[:, :, None] == jnp.arange(NODES, dtype=jnp.int32)[None, None, :]
    selected = (node_hot & kept).reshape(rows_here, FOLDS * NODES).astype(jnp.float32)
    weights = jnp.stack([grad * selected, hess * selected], axis=2).reshape(
        rows_here, FOLDS * NODES * 2
    )
    weights = weights.T.astype(jnp.bfloat16)
    local = accumulate(bins, weights)
    reduced = lax.psum_scatter(local, "rows", scatter_dimension=0, tiled=True)
    owned = reduced.shape[0] // 2
    split = reduced.reshape(owned, 2, feats, BINS)
    totals = jnp.sum(split[:, :, 0, :], axis=-1)
    running = jnp.cumsum(split, axis=-1)
    left_g, left_h = (running[:, 0], running[:, 1])
    whole_g = totals[:, 0][:, None, None]
    whole_h = totals[:, 1][:, None, None]
    gain = (
        left_g * left_g / (left_h + 1.0)
        + (whole_g - left_g) ** 2 / (whole_h - left_h + 1.0)
        - whole_g * whole_g / (whole_h + 1.0)
    )
    level = jnp.arange(BINS, dtype=jnp.int32)[None, None, :]
    gain = jnp.where(level < BINS - 1, gain, -1e30)
    mine = jnp.max(gain, axis=(1, 2))
    filled = jnp.full((FOLDS * NODES,), -1e30, jnp.float32)
    best = lax.dynamic_update_slice_in_dim(filled, mine, lax.axis_index("rows") * owned, 0)
    best = lax.pmax(best, "rows")
    best = lax.pmax(best, "feat")
    return (reduced, best.reshape(FOLDS, NODES))


def solution(mesh):
    in_specs = (P("feat", "rows"), P("rows"), P("rows", None), P("rows"), P("rows"))
    out_specs = (P("rows", "feat", None), P())
    return jax.shard_map(
        on_device, mesh=mesh, in_specs=in_specs, out_specs=out_specs, check_vma=False
    )
```

profile of v0, /device:TPU:0, one launch (start us, length us, event | category | flops | bytes accessed | tf_op | source)
XLA Modules:
  0.0 381.1 jit_solution(17522589929475790980)
XLA Ops:
  14.4 208.6 %while.24 = (s32[]{:T(128)}, f32[80,96,256]{2,0,1:T(8,128)}, bf16[80,4096]{1,0:T(8,128)(2,1)S(1)}, s32[96,4096]{1,0:T(8,128)}, s32[]{:T(128)}, /*index=5*/s32[]{...) while((s32[]{:T(128)}, f32[80,96,256]{2,0,1:T(8,128)}, ...), condition=%wide.region_1.2_spmd.clone.clone, body=%wide.region_0.1_spmd.clone.clone.sunk | while | flops 2027814912 | bytes 16810264 | solution.py:33
  23.7 4.2 %fusion.67 = f32[80,96,256]{2,0,1:T(8,128)} fusion(f32[80,96,256]{2,0,1:T(8,128)} %fusion.66, s32[16,512]{1,0:T(8,128)S(1)} %get-tuple-element.408, bf16[80,4096]{1,0:T(8,128)(2,1)S(1)} %get-tuple-element.440, s32[]{:T(128)S(6)} %select_n.25), kind=kOutput, calls=%fused_computation.26.clone.1 | convolution fusion | flops 337969152 | bytes 2736132 | tf_op jit(solution)/shard_map/while/body/eval_jaxpr/cr,fbr->cfb/dot_general | solution.py:26
  27.9 4.2 %fusion.68 = f32[80,96,256]{2,0,1:T(8,128)} fusion(f32[80,96,256]{2,0,1:T(8,128)} %fusion.67, s32[16,512]{1,0:T(8,128)S(1)} %get-tuple-element.409, bf16[80,4096]{1,0:T(8,128)(2,1)S(1)} %get-tuple-element.440, s32[]{:T(128)S(6)} %select_n.25), kind=kOutput, calls=%fused_computation.24.clone.1 | convolution fusion | flops 337969152 | bytes 2736132 | tf_op jit(solution)/shard_map/while/body/eval_jaxpr/cr,fbr->cfb/dot_general | solution.py:26
  32.1 4.2 %fusion.69 = f32[80,96,256]{2,0,1:T(8,128)} fusion(f32[80,96,256]{2,0,1:T(8,128)} %fusion.68, s32[16,512]{1,0:T(8,128)S(1)} %get-tuple-element.410, bf16[80,4096]{1,0:T(8,128)(2,1)S(1)} %get-tuple-element.440, s32[]{:T(128)S(6)} %select_n.25), kind=kOutput, calls=%fused_computation.22.clone.1 | convolution fusion | flops 337969152 | bytes 2736132 | tf_op jit(solution)/shard_map/while/body/eval_jaxpr/cr,fbr->cfb/dot_general | solution.py:26
  49.8 4.2 %fusion.67 = f32[80,96,256]{2,0,1:T(8,128)} fusion(f32[80,96,256]{2,0,1:T(8,128)} %fusion.66, s32[16,512]{1,0:T(8,128)S(1)} %get-tuple-element.408, bf16[80,4096]{1,0:T(8,128)(2,1)S(1)} %get-tuple-element.440, s32[]{:T(128)S(6)} %select_n.25), kind=kOutput, calls=%fused_computation.26.clone.1 | convolution fusion | flops 337969152 | bytes 2736132 | tf_op jit(solution)/shard_map/while/body/eval_jaxpr/cr,fbr->cfb/dot_general | solution.py:26
  54.0 4.2 %fusion.68 = f32[80,96,256]{2,0,1:T(8,128)} fusion(f32[80,96,256]{2,0,1:T(8,128)} %fusion.67, s32[16,512]{1,0:T(8,128)S(1)} %get-tuple-element.409, bf16[80,4096]{1,0:T(8,128)(2,1)S(1)} %get-tuple-element.440, s32[]{:T(128)S(6)} %select_n.25), kind=kOutput, calls=%fused_computation.24.clone.1 | convolution fusion | flops 337969152 | bytes 2736132 | tf_op jit(solution)/shard_map/while/body/eval_jaxpr/cr,fbr->cfb/dot_general | solution.py:26
  58.2 4.2 %fusion.69 = f32[80,96,256]{2,0,1:T(8,128)} fusion(f32[80,96,256]{2,0,1:T(8,128)} %fusion.68, s32[16,512]{1,0:T(8,128)S(1)} %get-tuple-element.410, bf16[80,4096]{1,0:T(8,128)(2,1)S(1)} %get-tuple-element.440, s32[]{:T(128)S(6)} %select_n.25), kind=kOutput, calls=%fused_computation.22.clone.1 | convolution fusion | flops 337969152 | bytes 2736132 | tf_op jit(solution)/shard_map/while/body/eval_jaxpr/cr,fbr->cfb/dot_general | solution.py:26
  80.0 4.2 %fusion.68 = f32[80,96,256]{2,0,1:T(8,128)} fusion(f32[80,96,256]{2,0,1:T(8,128)} %fusion.67, s32[16,512]{1,0:T(8,128)S(1)} %get-tuple-element.409, bf16[80,4096]{1,0:T(8,128)(2,1)S(1)} %get-tuple-element.440, s32[]{:T(128)S(6)} %select_n.25), kind=kOutput, calls=%fused_computation.24.clone.1 | convolution fusion | flops 337969152 | bytes 2736132 | tf_op jit(solution)/shard_map/while/body/eval_jaxpr/cr,fbr->cfb/dot_general | solution.py:26
  84.2 4.2 %fusion.69 = f32[80,96,256]{2,0,1:T(8,128)} fusion(f32[80,96,256]{2,0,1:T(8,128)} %fusion.68, s32[16,512]{1,0:T(8,128)S(1)} %get-tuple-element.410, bf16[80,4096]{1,0:T(8,128)(2,1)S(1)} %get-tuple-element.440, s32[]{:T(128)S(6)} %select_n.25), kind=kOutput, calls=%fused_computation.22.clone.1 | convolution fusion | flops 337969152 | bytes 2736132 | tf_op jit(solution)/shard_map/while/body/eval_jaxpr/cr,fbr->cfb/dot_general | solution.py:26
  106.1 4.2 %fusion.68 = f32[80,96,256]{2,0,1:T(8,128)} fusion(f32[80,96,256]{2,0,1:T(8,128)} %fusion.67, s32[16,512]{1,0:T(8,128)S(1)} %get-tuple-element.409, bf16[80,4096]{1,0:T(8,128)(2,1)S(1)} %get-tuple-element.440, s32[]{:T(128)S(6)} %select_n.25), kind=kOutput, calls=%fused_computation.24.clone.1 | convolution fusion | flops 337969152 | bytes 2736132 | tf_op jit(solution)/shard_map/while/body/eval_jaxpr/cr,fbr->cfb/dot_general | solution.py:26
  110.3 4.2 %fusion.69 = f32[80,96,256]{2,0,1:T(8,128)} fusion(f32[80,96,256]{2,0,1:T(8,128)} %fusion.68, s32[16,512]{1,0:T(8,128)S(1)} %get-tuple-element.410, bf16[80,4096]{1,0:T(8,128)(2,1)S(1)} %get-tuple-element.440, s32[]{:T(128)S(6)} %select_n.25), kind=kOutput, calls=%fused_computation.22.clone.1 | convolution fusion | flops 337969152 | bytes 2736132 | tf_op jit(solution)/shard_map/while/body/eval_jaxpr/cr,fbr->cfb/dot_general | solution.py:26
  132.2 4.2 %fusion.68 = f32[80,96,256]{2,0,1:T(8,128)} fusion(f32[80,96,256]{2,0,1:T(8,128)} %fusion.67, s32[16,512]{1,0:T(8,128)S(1)} %get-tuple-element.409, bf16[80,4096]{1,0:T(8,128)(2,1)S(1)} %get-tuple-element.440, s32[]{:T(128)S(6)} %select_n.25), kind=kOutput, calls=%fused_computation.24.clone.1 | convolution fusion | flops 337969152 | bytes 2736132 | tf_op jit(solution)/shard_map/while/body/eval_jaxpr/cr,fbr->cfb/dot_general | solution.py:26
  136.4 4.2 %fusion.69 = f32[80,96,256]{2,0,1:T(8,128)} fusion(f32[80,96,256]{2,0,1:T(8,128)} %fusion.68, s32[16,512]{1,0:T(8,128)S(1)} %get-tuple-element.410, bf16[80,4096]{1,0:T(8,128)(2,1)S(1)} %get-tuple-element.440, s32[]{:T(128)S(6)} %select_n.25), kind=kOutput, calls=%fused_computation.22.clone.1 | convolution fusion | flops 337969152 | bytes 2736132 | tf_op jit(solution)/shard_map/while/body/eval_jaxpr/cr,fbr->cfb/dot_general | solution.py:26
  158.2 4.2 %fusion.68 = f32[80,96,256]{2,0,1:T(8,128)} fusion(f32[80,96,256]{2,0,1:T(8,128)} %fusion.67, s32[16,512]{1,0:T(8,128)S(1)} %get-tuple-element.409, bf16[80,4096]{1,0:T(8,128)(2,1)S(1)} %get-tuple-element.440, s32[]{:T(128)S(6)} %select_n.25), kind=kOutput, calls=%fused_computation.24.clone.1 | convolution fusion | flops 337969152 | bytes 2736132 | tf_op jit(solution)/shard_map/while/body/eval_jaxpr/cr,fbr->cfb/dot_general | solution.py:26
  162.5 4.2 %fusion.69 = f32[80,96,256]{2,0,1:T(8,128)} fusion(f32[80,96,256]{2,0,1:T(8,128)} %fusion.68, s32[16,512]{1,0:T(8,128)S(1)} %get-tuple-element.410, bf16[80,4096]{1,0:T(8,128)(2,1)S(1)} %get-tuple-element.440, s32[]{:T(128)S(6)} %select_n.25), kind=kOutput, calls=%fused_computation.22.clone.1 | convolution fusion | flops 337969152 | bytes 2736132 | tf_op jit(solution)/shard_map/while/body/eval_jaxpr/cr,fbr->cfb/dot_general | solution.py:26
  184.3 4.2 %fusion.68 = f32[80,96,256]{2,0,1:T(8,128)} fusion(f32[80,96,256]{2,0,1:T(8,128)} %fusion.67, s32[16,512]{1,0:T(8,128)S(1)} %get-tuple-element.409, bf16[80,4096]{1,0:T(8,128)(2,1)S(1)} %get-tuple-element.440, s32[]{:T(128)S(6)} %select_n.25), kind=kOutput, calls=%fused_computation.24.clone.1 | convolution fusion | flops 337969152 | bytes 2736132 | tf_op jit(solution)/shard_map/while/body/eval_jaxpr/cr,fbr->cfb/dot_general | solution.py:26
  188.5 4.2 %fusion.69 = f32[80,96,256]{2,0,1:T(8,128)} fusion(f32[80,96,256]{2,0,1:T(8,128)} %fusion.68, s32[16,512]{1,0:T(8,128)S(1)} %get-tuple-element.410, bf16[80,4096]{1,0:T(8,128)(2,1)S(1)} %get-tuple-element.440, s32[]{:T(128)S(6)} %select_n.25), kind=kOutput, calls=%fused_computation.22.clone.1 | convolution fusion | flops 337969152 | bytes 2736132 | tf_op jit(solution)/shard_map/while/body/eval_jaxpr/cr,fbr->cfb/dot_general | solution.py:26
  210.4 4.2 %fusion.68 = f32[80,96,256]{2,0,1:T(8,128)} fusion(f32[80,96,256]{2,0,1:T(8,128)} %fusion.67, s32[16,512]{1,0:T(8,128)S(1)} %get-tuple-element.409, bf16[80,4096]{1,0:T(8,128)(2,1)S(1)} %get-tuple-element.440, s32[]{:T(128)S(6)} %select_n.25), kind=kOutput, calls=%fused_computation.24.clone.1 | convolution fusion | flops 337969152 | bytes 2736132 | tf_op jit(solution)/shard_map/while/body/eval_jaxpr/cr,fbr->cfb/dot_general | solution.py:26
  214.6 4.2 %fusion.69 = f32[80,96,256]{2,0,1:T(8,128)} fusion(f32[80,96,256]{2,0,1:T(8,128)} %fusion.68, s32[16,512]{1,0:T(8,128)S(1)} %get-tuple-element.410, bf16[80,4096]{1,0:T(8,128)(2,1)S(1)} %get-tuple-element.440, s32[]{:T(128)S(6)} %select_n.25), kind=kOutput, calls=%fused_computation.22.clone.1 | convolution fusion | flops 337969152 | bytes 2736132 | tf_op jit(solution)/shard_map/while/body/eval_jaxpr/cr,fbr->cfb/dot_general | solution.py:26
  223.0 10.9 %copy.28 = f32[80,96,256]{2,1,0:T(8,128)} copy(f32[80,96,256]{2,0,1:T(8,128)} %get-tuple-element.318) | data formatting | bytes 15728640 | tf_op jit(solution)/shard_map/while | solution.py:33
  234.0 86.0 %reduce-scatter.2.cloned.1.call-done = f32[20,96,256]{2,1,0:T(8,128)} async-done(((f32[80,96,256]{2,1,0:T(8,128)}), f32[20,96,256]{2,1,0:T(8,128)}) %reduce-scatter.2.cloned.1.call-update) | async-done | bytes 1966096 | tf_op jit(solution)/shard_map/reduce_scatter | solution.py:48
  324.9 22.4 %reduce-window.6 = f32[10,2,96,2,128]{4,2,3,1,0:T(8,128)S(1)} reduce-window(f32[10,2,96,2,128]{4,2,3,1,0:T(8,128)} %copy.29, f32[]{:T(128)} %constant.393.clone.1), window={size=1x1x1x1x128 pad=0_0x0_0x0_0x0_0x127_0}, to_apply=%region_3.4 | reduce-window | flops 62423040 | bytes 3932164 | tf_op jit(solution)/shard_map/reduce-window
  350.1 8.9 %pmax.14 = f32[40]{0:T(128)S(1)} all-reduce(f32[40]{0:T(128)S(1)} %dynamic_update_slice.3), channel_id=1, replica_groups=mesh['rows'=4,'feat'=8] {'rows'}, use_global_device_ids=true, to_apply=%region_7.0 | all-reduce | flops 40 | bytes 320 | tf_op jit(solution)/shard_map/pmax | solution.py:66
  359.1 14.4 %pmax.15 = f32[10,4]{1,0:T(8,128)S(1)} all-reduce(f32[10,4]{1,0:T(8,128)S(1)} %reshape.551), channel_id=1, replica_groups=mesh['rows'=4,'feat'=8] {'feat'}, use_global_device_ids=true, to_apply=%region_8.0 | all-reduce | flops 40 | bytes 320 | tf_op jit(solution)/shard_map/pmax | solution.py:67
  (74 shorter events, 148.3 us)
Async XLA Ops:
  7.2 1.4 copy-start
  7.2 1.8 copy-start.1
  7.2 2.1 copy-start.2
  7.2 312.7 %reduce-scatter.2.cloned.1.call-start = ((), (), s32[]{:S(2)}) async-start(), calls=%async_computation.1 | async-start | bytes 9830400 | tf_op jit(solution)/shard_map/reduce_scatter | solution.py:48
Sparse Core Ops, SparseCore 0:
  234.1 85.8 reduce-scatter.1
where the time goes:
time: 385 us; the launch traced here: 381 us
  matrix products  202 us (52%)
  waiting for transfers between devices  86 us (22%)
  local copies, waits for them, and re-layouts  30.7 us (8%)
  other arithmetic  25.1 us (7%)
  blocking collectives  23.3 us (6%)
  between operations  14.2 us (4%)
    dot_general x48, matrix products, visit(): jnp.einsum('cr,fbr->cfb', part_weights, onehot, preferred_element_type=jn...  202 us
    reduce_scatter x1, waiting for transfers between devices, on_device(): reduced = lax.psum_scatter(local, 'rows', scatter_dimension=0, tiled=True)  86 us
    another operation x5, other arithmetic  23.4 us
    pmax x1, blocking collectives, on_device(): best = lax.pmax(best, 'feat')  14.4 us
    while x1, local copies, waits for them, and re-layouts, accumulate(): return lax.fori_loop(0, rows_here // block, visit, empty)  10.9 us
    pmax x1, blocking collectives, on_device(): best = lax.pmax(best, 'rows')  8.91 us
  transfers between devices with their start and end apart: 1, of which 1 were waited for; matrix products, arithmetic and copies ran while one was open for 0% of the time, Pallas kernels for 0%

commit v1 on v0

v1 whole, which is shorter than its diff:
```python
import functools

import jax
import jax.numpy as jnp
from jax import lax
from jax.experimental import pallas as pl
from jax.experimental.pallas import tpu as pltpu
from jax.sharding import PartitionSpec as P


BINS = 256
FOLDS = 10
NODES = 4
PAIRS = FOLDS * NODES
COLS = 2 * PAIRS
TILE = 256
F8 = jnp.float8_e4m3fn
F32 = jnp.float32
BF16 = jnp.bfloat16


VMEM = pl.BlockSpec(memory_space=pltpu.VMEM)
SMEM = pl.BlockSpec(memory_space=pltpu.SMEM)
ANY = pl.BlockSpec(memory_space=pl.ANY)


def params():
    return pltpu.CompilerParams(vmem_limit_bytes=16 * 2**20)


def cost(flops, bytes_accessed=1 << 20):
    return pl.CostEstimate(
        flops=int(flops), bytes_accessed=int(bytes_accessed), transcendentals=0
    )


def weight_lines(low, high):
    shape = low.shape
    line = lax.broadcasted_iota(jnp.int32, shape, 0)
    node = (line % NODES).astype(F32)
    first = line < NODES
    fold = high[2:3]
    grads, hesss = [], []
    for j in range(FOLDS // 2):
        source, at = (low, 2 * j) if j < 4 else (high, 0)
        placed = jnp.where(first, source[at : at + 1], source[at + 1 : at + 2])
        k = jnp.where(first, F32(2 * j), F32(2 * j + 1))
        chosen = (placed == node) & (fold != k)
        grads.append(jnp.where(chosen, high[3:4], F32(0)))
        hesss.append(jnp.where(chosen, high[4:5], F32(0)))
    return jnp.concatenate(grads + hesss, axis=0).astype(BF16)


def one_hot(row, levels):
    packed = jnp.broadcast_to(row, (16, TILE)).astype(BF16)
    hit = jnp.concatenate([packed] * (BINS // 16), axis=0) == levels
    return jnp.where(hit, jnp.ones((), F8), jnp.zeros((), F8))


def bin_levels():
    return lax.broadcasted_iota(jnp.int32, (BINS, TILE), 0).astype(BF16)


def accumulate_pair(accs, feature, sources, levels):
    turn = 0
    for bins, line, weights, column, rows in sources:
        for at in range(0, rows, TILE):
            lhs = weights[:, pl.ds(column + at, TILE)]
            for q, acc in enumerate(accs):
                row = bins[pl.ds(line + feature + q, 1), pl.ds(at, TILE)]
                pltpu.matmul_push_rhs(
                    one_hot(row, levels), staging_register=turn % 2, mxu_index=q, transpose=True
                )
                pltpu.matmul_acc_lhs(acc, lhs, load_staged_rhs=turn % 2)
            turn += 1


def prepare_kernel(group, owned, size, me, parity, bins, nodes, fold, gradient, hessian, *refs):
    first, later = refs[: group - 1], refs[group - 1 : -2]
    own, rowdata = refs[-2:]
    rows = bins.shape[1]
    rowdata[0:FOLDS] = nodes[...].astype(F32)
    rowdata[FOLDS + 3 :] = jnp.zeros((16 - FOLDS - 3, rows), F32)
    for i, ref in enumerate((fold, gradient, hessian)):
        lines = ref[...].astype(F32)
        for j in range(rows // 128):
            rowdata[FOLDS + i : FOLDS + i + 1, j * 128 : j * 128 + 128] = lines[j : j + 1]

    def move(to, at, source, count):
        if owned % 8 == 0:
            to[at : at + count] = bins[pl.ds(pl.multiple_of(source, 8), count)].astype(F32)
        else:
            for i in range(count):
                to[at + i : at + i + 1] = bins[pl.ds(source + i, 1)].astype(F32)

    for d in range(1, group):
        base = (me[0] ^ d) * owned
        first[d - 1][0:8] = rowdata[pl.ds(pl.multiple_of(parity[0] * 8, 8), 8)]
        move(first[d - 1], 8, base, size)
        if later:
            move(later[d - 1], 0, base + size, owned - size)
    move(own, 0, me[0] * owned, owned)


def prepare(me, parity, bins, nodes, fold, gradient, hessian, group, owned, size):
    rows = bins.shape[1]
    shapes = [(size + 8, rows)] * (group - 1)
    if owned > size:
        shapes += [(owned - size, rows)] * (group - 1)
    shapes += [(owned, rows), (16, rows)]
    wide = (rows // 128, 128)
    out = pl.pallas_call(
        functools.partial(prepare_kernel, group, owned, size),
        out_shape=[jax.ShapeDtypeStruct(shape, F32) for shape in shapes],
        in_specs=[SMEM, SMEM] + [VMEM] * 5,
        out_specs=[VMEM] * len(shapes),
        compiler_params=params(),
        cost_estimate=cost(1 << 30),
        name="prepare",
    )(me, parity, bins, nodes.T, fold.reshape(wide), gradient.reshape(wide), hessian.reshape(wide))
    return out[: group - 1], out[group - 1 : -2], out[-2], out[-1]


def own_kernel(bins, rowdata, *refs):
    outs, weights = refs[:-1], refs[-1]
    feats, rows = bins.shape
    size = feats // len(outs)

    def prepare(i, carry):
        at = pl.ds(pl.multiple_of(i * 512, 512), 512)
        weights[:, at] = weight_lines(rowdata[0:8, at], rowdata[8:16, at])
        return carry

    lax.fori_loop(0, rows // 512, prepare, 0)
    levels = bin_levels()

    def body(acc0, acc1):
        for c, out in enumerate(outs):

            def visit(p, carry, c=c, out=out):
                accumulate_pair((acc0, acc1), 2 * p, [(bins, c * size, weights, 0, rows)], levels)
                for q, acc in enumerate((acc0, acc1)):
                    at = pl.ds(pl.multiple_of((2 * p + q) * COLS, COLS), COLS)
                    out[at] = pltpu.matmul_pop(acc)
                return carry

            lax.fori_loop(0, size // 2, visit, 0)

    pl.run_scoped(body, pltpu.ACC(0)((COLS, BINS), F32), pltpu.ACC(1)((COLS, BINS), F32))


def own_part(bins, rowdata, size):
    feats, rows = bins.shape
    out = jax.ShapeDtypeStruct((size * COLS, BINS), F32)
    return pl.pallas_call(
        own_kernel,
        out_shape=[out] * (feats // size),
        in_specs=[VMEM, VMEM],
        out_specs=[VMEM] * (feats // size),
        scratch_shapes=[pltpu.VMEM((COLS, rows), BF16)],
        compiler_params=params(),
        cost_estimate=cost(2 * feats * rows * COLS * BINS),
        name="own_part",
    )(bins, rowdata)


def weights_kernel(count, rows, parity, *refs):
    mine, other, out = refs[:count], refs[count], refs[count + 1]
    even = parity[0] == 0
    for s in range(count):

        def prepare(i, carry, s=s):
            at = pl.ds(pl.multiple_of(i * 512, 512), 512)
            a = mine[s][0:8, at]
            b = other[8 * s : 8 * s + 8, at]
            to = pl.ds(pl.multiple_of(s * rows + i * 512, 512), 512)
            out[:, to] = weight_lines(jnp.where(even, a, b), jnp.where(even, b, a))
            return carry

        lax.fori_loop(0, rows // 512, prepare, 0)


def remote_weights(parity, mine, other):
    count = len(mine)
    rows = other.shape[1]
    return pl.pallas_call(
        functools.partial(weights_kernel, count, rows),
        out_shape=jax.ShapeDtypeStruct((COLS, count * rows), BF16),
        in_specs=[SMEM] + [VMEM] * (count + 1),
        out_specs=VMEM,
        compiler_params=params(),
        cost_estimate=cost(1 << 30),
        name="remote_weights",
    )(parity, *mine, other)


def chunk_kernel(count, group, line, feats, rows, final, me, part, best_in, weights, *refs):
    bins, pieces, best_out, held = refs[:count], refs[count:-2], refs[-2], refs[-1]
    levels = bin_levels()
    lower = lax.broadcasted_iota(jnp.int32, (BINS, BINS), 0)
    upper = lax.broadcasted_iota(jnp.int32, (BINS, BINS), 1)
    triangle = (lower <= upper).astype(BF16)
    last = lax.broadcasted_iota(jnp.int32, (PAIRS, BINS), 1) == BINS - 1
    sources = [(bins[s], line, weights, s * rows, rows) for s in range(count)]

    def body(acc0, acc1):
        accs = (acc0, acc1)

        def visit(p, carry):
            accumulate_pair(accs, 2 * p, sources, levels)
            for q, acc in enumerate(accs):
                at = pl.ds(pl.multiple_of((2 * p + q) * COLS, COLS), COLS)
                whole = pltpu.matmul_pop(acc) + part[at]
                for half in range(2):
                    held[half, at] = whole[:, half * 128 : half * 128 + 128]
            return carry

        lax.fori_loop(0, feats // 2, visit, 0)

        best = best_in[...]
        for p in range(feats // 2):
            for q, acc in enumerate(accs):
                f = 2 * p + q
                if p == 0:
                    pltpu.matmul_push_rhs(triangle, staging_register=0, mxu_index=q)
                at = slice(f * COLS, (f + 1) * COLS)
                rest = jnp.concatenate([held[0, at], held[1, at]], axis=1)
                for piece in range(3):
                    high = rest.astype(BF16)
                    rest = rest - high.astype(F32)
                    pltpu.matmul_acc_lhs(
                        acc, high, load_staged_rhs=0 if p == 0 and piece == 0 else None
                    )
            for acc in accs:
                left = pltpu.matmul_pop(acc)
                gl, hl = left[:PAIRS], left[PAIRS:]
                g, h = gl[:, BINS - 1 :], hl[:, BINS - 1 :]
                gain = (
                    gl * gl / (hl + 1.0)
                    + (g - gl) * (g - gl) / (h - hl + 1.0)
                    - g * g / (h + 1.0)
                )
                best = jnp.maximum(best, jnp.where(last, F32(-3e38), gain))
        if final:
            best = jnp.broadcast_to(jnp.max(best, axis=1, keepdims=True), (PAIRS, 128))
        best_out[...] = best

    pl.run_scoped(body, pltpu.ACC(0)((COLS, BINS), F32), pltpu.ACC(1)((COLS, BINS), F32))

    share = COLS // group
    for d in range(group):
        for j in range(share):
            row = (j % 2) * PAIRS + (me[0] ^ d) * (share // 2) + j // 2
            for half in range(2):
                pieces[d][j, :, half * 128 : half * 128 + 128] = held[
                    half, pl.ds(row, feats, stride=COLS), :
                ]


def chunk(me, part, best, weights, bins, line, feats, group, final):
    count = len(bins)
    rows = weights.shape[1] // count
    share = COLS // group
    piece = jax.ShapeDtypeStruct((share, feats, BINS), F32)
    out = pl.pallas_call(
        functools.partial(chunk_kernel, count, group, line, feats, rows, final),
        out_shape=[piece] * group + [jax.ShapeDtypeStruct((PAIRS, 128 if final else BINS), F32)],
        in_specs=[SMEM, VMEM, VMEM, VMEM] + [VMEM] * count,
        out_specs=[VMEM] * (group + 1),
        scratch_shapes=[pltpu.VMEM((2, feats * COLS, 128), F32)],
        compiler_params=params(),
        cost_estimate=cost(2 * feats * rows * count * COLS * BINS),
        name="chunk",
    )(me, part, best, weights, *bins)
    return out[:-1], out[-1]


def place_kernel(group, first, owned, feats, me, *refs):
    pieces, out, sems = refs[:group], refs[-2], refs[-1]
    copies = []
    for d in range(group):
        at = pl.multiple_of((me[0] ^ d) * owned + first, 8)
        copies.append(
            pltpu.make_async_copy(pieces[d], out.at[:, pl.ds(at, feats), :], sems.at[d])
        )
    for copy in copies:
        copy.start()
    for copy in copies:
        copy.wait()


def place(me, held, pieces, first, owned, shape):
    group = len(pieces)
    feats = pieces[0].shape[1]
    if owned % 8 or first % 8 or feats % 8:
        if held is None:
            held = jnp.zeros(shape, F32)
        for d, piece in enumerate(pieces):
            held = lax.dynamic_update_slice_in_dim(held, piece, (me[0] ^ d) * owned + first, 1)
        return held
    return pl.pallas_call(
        functools.partial(place_kernel, group, first, owned, feats),
        out_shape=jax.ShapeDtypeStruct(shape, F32),
        in_specs=[SMEM] + [VMEM] * group + ([] if held is None else [ANY]),
        out_specs=ANY,
        scratch_shapes=[pltpu.SemaphoreType.DMA((group,))],
        input_output_aliases={} if held is None else {group + 1: 0},
        compiler_params=params(),
        name="place",
    )(me, *pieces, *([] if held is None else [held]))


def on_device(group, feat_size, bins, fold, nodes, gradient, hessian):
    feats, _ = bins.shape
    owned = feats // group
    size = 8 if owned % 8 == 0 else owned
    chunks = owned // size
    me = lax.axis_index("rows")[None]
    parity = (lax.axis_index("feat") & 1)[None]
    others = range(1, group)

    def swap(x, axis, count, d):
        return lax.ppermute(x, axis, [(i, i ^ d) for i in range(count)])

    first, later, own, rowdata = prepare(
        me, parity, bins, nodes, fold, gradient, hessian, group, owned, size
    )
    arrived = [swap(first[d - 1], "rows", group, d) for d in others]
    if later:
        later = [swap(later[d - 1], "rows", group, d) for d in others]
    part = own_part(own, rowdata, size)
    traded = swap(jnp.concatenate([a[:8] for a in arrived]), "feat", feat_size, 1)
    weights = remote_weights(parity, arrived, traded)
    best = jnp.full((PAIRS, BINS), -3e38, F32)
    received = []
    for c in range(chunks):
        left = chunks - 1 - c
        source, line = (arrived, 8) if c == 0 else (later, (c - 1) * size)
        pieces, best = chunk(
            me, part[c], best, weights, source, line, size, group, left == 0
        )
        received.append([pieces[0]] + [swap(pieces[d], "rows", group, d) for d in others])
    step = 1
    while step < feat_size:
        best = jnp.maximum(best, swap(best, "feat", feat_size, step))
        step *= 2
    tops = [swap(best, "rows", group, d) for d in others]
    out = None
    for c, pieces in enumerate(received):
        out = place(me, out, pieces, c * size, owned, (COLS // group, feats, BINS))
    for top in tops:
        best = jnp.maximum(best, top)
    return out, best[:, 0].reshape(FOLDS, NODES)


def solution(mesh):
    in_specs = (P("feat", "rows"), P("rows"), P("rows", None), P("rows"), P("rows"))
    out_specs = (P("rows", "feat", None), P())
    group = mesh.shape["rows"]

    def step(*args):
        return on_device(group, mesh.shape["feat"], *args)

    return jax.shard_map(
        step, mesh=mesh, in_specs=in_specs, out_specs=out_specs, check_vma=False
    )
```

time: 385 us -> 107 us (0.28)
  matrix products: 202 us -> 0 us
  waiting for transfers between devices: 86 us -> 30 us
  Pallas kernels: 0 us -> 44.1 us
  starting transfers between devices: 0.04 us -> 26.4 us
  local copies, waits for them, and re-layouts: 30.7 us -> 5.25 us
  other arithmetic: 25.1 us -> 0.15 us
  blocking collectives: 23.3 us -> 0 us
  between operations: 14.2 us -> 0.83 us
    dot_general x48 -> x0, matrix products: 202 us -> none  [visit(): jnp.einsum('cr,fbr->cfb', part_weights, onehot, preferred_element_type=jn...]
    reduce_scatter x1 -> x0, waiting for transfers between devices: 86 us -> none  [on_device(): reduced = lax.psum_scatter(local, 'rows', scatter_dimension=0, tiled=True)]
    pallas_call x0 -> x9, Pallas kernels: none -> 44.1 us  [the longest x3 30.2 us: chunk(): pl.pallas_call(functools.partial(chunk_kernel, count, group, line, feats,...]
    ppermute x0 -> x22, waiting for transfers between devices: none -> 30 us  [swap(): return lax.ppermute(x, axis, [(i, i ^ d) for i in range(count)])]
    ppermute x0 -> x22, starting transfers between devices: none -> 26.4 us  [swap(): return lax.ppermute(x, axis, [(i, i ^ d) for i in range(count)])]
    another operation x6 -> x0, other arithmetic: 23.4 us -> none
    pmax x2 -> x0, blocking collectives: 23.3 us -> none  [the longest x1 14.4 us: on_device(): best = lax.pmax(best, 'feat')]
    while x1 -> x0, local copies, waits for them, and re-layouts: 10.9 us -> none  [accumulate(): return lax.fori_loop(0, rows_here // block, visit, empty)]
  transfers between devices with their start and end apart: 1 -> 22, of which waited for: 1 -> 10; matrix products, arithmetic and copies ran while one was open for 0% -> 1% of each run, Pallas kernels for 0% -> 31%
where the time goes in v1:
time: 107 us
  Pallas kernels  44.1 us (41%)
  waiting for transfers between devices  30 us (28%)
  starting transfers between devices  26.4 us (25%)
  local copies, waits for them, and re-layouts  5.25 us (5%)
    pallas_call x3, Pallas kernels, chunk(): pl.pallas_call(functools.partial(chunk_kernel, count, group, line, feats,...  30.2 us
    ppermute x22, waiting for transfers between devices, swap(): return lax.ppermute(x, axis, [(i, i ^ d) for i in range(count)])  30 us
    ppermute x22, starting transfers between devices, swap(): return lax.ppermute(x, axis, [(i, i ^ d) for i in range(count)])  26.4 us
    pallas_call x1, Pallas kernels, own_part(): pl.pallas_call(own_kernel, out_shape=[out] * (feats // size), in_specs=[V...  10.4 us
    unnamed x11, local copies, waits for them, and re-layouts  5.14 us
    pallas_call x3, Pallas kernels, place(): pl.pallas_call(functools.partial(place_kernel, group, first, owned, feats...  2.59 us
  transfers between devices with their start and end apart: 22, of which 10 were waited for; matrix products, arithmetic and copies ran while one was open for 1% of the time, Pallas kernels for 31%

profile of v1, /device:TPU:0, one launch (start us, length us, event | category | flops | bytes accessed | tf_op | source)
XLA Modules:
  0.0 106.8 jit_solution(3169364571123285778)
XLA Ops:
  0.6 1.4 %copy-done = s32[96,4096]{1,0:T(8,128)S(1)} copy-done((s32[96,4096]{1,0:T(8,128)S(1)}, s32[96,4096]{1,0:T(8,128)}, u32[]{:S(2)}) %copy-start) | copy-done | bytes 1572888
  5.3 3.0 %collective-permute-start = (f32[16,4096]{1,0:T(8,128)S(1)}, f32[16,4096]{1,0:T(8,128)S(1)}, u32[]{:S(2)}, u32[]{:S(2)}) collective-permute-start(f32[16,4096]{1,0:T(8,128)S(1)} %get-tuple-element.33), channel_id=1, source_target_pairs={{0,8},{8,0},{16,24},{24,16},{1,9},{9,1},{17,25},{25,17},{2,10},{10... | collective-permute-start | bytes 786440 | tf_op jit(solution)/shard_map/ppermute | solution.py:323
  8.3 1.5 %collective-permute-start.1 = (f32[16,4096]{1,0:T(8,128)S(1)}, f32[16,4096]{1,0:T(8,128)S(1)}, u32[]{:S(2)}, u32[]{:S(2)}) collective-permute-start(f32[16,4096]{1,0:T(8,128)S(1)} %get-tuple-element.34), channel_id=1, source_target_pairs={{0,16},{8,24},{16,0},{24,8},{1,17},{9,25},{17,1},{25,9},{2,18},{10... | collective-permute-start | bytes 786440 | tf_op jit(solution)/shard_map/ppermute | solution.py:323
  9.9 5.6 %collective-permute-done.refs_0_ = f32[16,4096]{1,0:T(8,128)S(1)} collective-permute-done((f32[16,4096]{1,0:T(8,128)S(1)}, f32[16,4096]{1,0:T(8,128)S(1)}, u32[]{:S(2)}, u32[]{:S(2)}) %collective-permute-start) | collective-permute-done | bytes 262176 | tf_op jit(solution)/shard_map/ppermute | solution.py:323
  15.5 6.2 %collective-permute-done.1.refs_1_ = f32[16,4096]{1,0:T(8,128)S(1)} collective-permute-done((f32[16,4096]{1,0:T(8,128)S(1)}, f32[16,4096]{1,0:T(8,128)S(1)}, u32[]{:S(2)}, u32[]{:S(2)}) %collective-permute-start.1) | collective-permute-done | bytes 262176 | tf_op jit(solution)/shard_map/ppermute | solution.py:323
  21.9 1.3 %collective-permute-start.4 = (f32[16,4096]{1,0:T(8,128)S(1)}, f32[16,4096]{1,0:T(8,128)S(1)}, u32[]{:S(2)}, u32[]{:S(2)}) collective-permute-start(f32[16,4096]{1,0:T(8,128)S(1)} %get-tuple-element.37), channel_id=1, source_target_pairs={{0,8},{8,0},{16,24},{24,16},{1,9},{9,1},{17,25},{25,17},{2,10},{10... | collective-permute-start | bytes 786440 | tf_op jit(solution)/shard_map/ppermute | solution.py:323
  24.0 1.4 %collective-permute-start.6 = (f32[16,4096]{1,0:T(8,128)S(1)}, f32[16,4096]{1,0:T(8,128)S(1)}, u32[]{:S(2)}, u32[]{:S(2)}) collective-permute-start(f32[16,4096]{1,0:T(8,128)S(1)} %get-tuple-element.39), channel_id=1, source_target_pairs={{0,24},{8,16},{16,8},{24,0},{1,25},{9,17},{17,9},{25,1},{2,26},{10... | collective-permute-start | bytes 786440 | tf_op jit(solution)/shard_map/ppermute | solution.py:323
  25.4 10.4 %own_part.1 = (f32[640,256]{1,0:T(8,128)S(1)}, f32[640,256]{1,0:T(8,128)S(1)}, f32[640,256]{1,0:T(8,128)S(1)}) custom-call(f32[24,4096]{1,0:T(8,128)S(1)} %get-tuple-element.28.bins, f32[16,4096]{1,0:T(8,128)S(1)} %get-tuple-element.29.rowdata), custom_call_target="tpu_custom_call" | custom-call | flops 4026531840 | bytes 1048576 | tf_op jit(solution)/shard_map/own_part/pallas_call | solution.py:155
  36.7 10.0 %chunk.3 = (f32[20,8,256]{2,1,0:T(8,128)S(1)}, f32[20,8,256]{2,1,0:T(8,128)S(1)}, f32[20,8,256]{2,1,0:T(8,128)S(1)}, f32[20,8,256]{2,1,0:T(8,128)S(1)}, f32[40,256]{1,0:T(8,128)S(1)}) custom-call(s32[1]{0:T(128)} %bitcast.me, f32[640,256]{1,0:T(8,128)S(1)} %get-tuple-element.32.part, f32[40,256]{1,0:T(8,128)S(1)} %broadcast_in_dim.11.best_in, ...), custom_call_target="tpu_custom_call" | custom-call | flops 4026531840 | bytes 1048576 | tf_op jit(solution)/shard_map/chunk/pallas_call | solution.py:265
  46.7 10.1 %chunk.4 = (f32[20,8,256]{2,1,0:T(8,128)S(1)}, f32[20,8,256]{2,1,0:T(8,128)S(1)}, f32[20,8,256]{2,1,0:T(8,128)S(1)}, f32[20,8,256]{2,1,0:T(8,128)S(1)}, f32[40,256]{1,0:T(8,128)S(1)}) custom-call(s32[1]{0:T(128)} %bitcast.me, f32[640,256]{1,0:T(8,128)S(1)} %get-tuple-element.31.part, f32[40,256]{1,0:T(8,128)S(1)} %get-tuple-element.36.best_in, ...), custom_call_target="tpu_custom_call" | custom-call | flops 4026531840 | bytes 1048576 | tf_op jit(solution)/shard_map/chunk/pallas_call | solution.py:265
  56.8 1.3 %collective-permute-start.10 = (f32[20,8,256]{2,1,0:T(8,128)S(1)}, f32[20,8,256]{2,1,0:T(8,128)S(1)}, u32[]{:S(2)}, u32[]{:S(2)}) collective-permute-start(f32[20,8,256]{2,1,0:T(8,128)S(1)} %get-tuple-element.46), channel_id=1, source_target_pairs={{0,8},{8,0},{16,24},{24,16},{1,9},{9,1},{17,25},{25,17},{2,10},{10... | collective-permute-start | bytes 491528 | tf_op jit(solution)/shard_map/ppermute | solution.py:323
  58.9 1.5 %collective-permute-start.14 = (f32[20,8,256]{2,1,0:T(8,128)S(1)}, f32[20,8,256]{2,1,0:T(8,128)S(1)}, u32[]{:S(2)}, u32[]{:S(2)}) collective-permute-start(f32[20,8,256]{2,1,0:T(8,128)S(1)} %get-tuple-element.51), channel_id=1, source_target_pairs={{0,16},{8,24},{16,0},{24,8},{1,17},{9,25},{17,1},{25,9},{2,18},{10... | collective-permute-start | bytes 491528 | tf_op jit(solution)/shard_map/ppermute | solution.py:323
  61.5 10.1 %chunk.5 = (f32[20,8,256]{2,1,0:T(8,128)S(1)}, f32[20,8,256]{2,1,0:T(8,128)S(1)}, f32[20,8,256]{2,1,0:T(8,128)S(1)}, f32[20,8,256]{2,1,0:T(8,128)S(1)}, f32[40,128]{1,0:T(8,128)S(1)}) custom-call(s32[1]{0:T(128)} %bitcast.me, f32[640,256]{1,0:T(8,128)S(1)} %get-tuple-element.30.part, f32[40,256]{1,0:T(8,128)S(1)} %get-tuple-element.40.best_in, ...), custom_call_target="tpu_custom_call" | custom-call | flops 4026531840 | bytes 1048576 | tf_op jit(solution)/shard_map/chunk/pallas_call | solution.py:265
  72.9 1.6 %collective-permute-start.17 = (f32[40,128]{1,0:T(8,128)S(1)}, f32[40,128]{1,0:T(8,128)S(1)}, u32[]{:S(2)}, u32[]{:S(2)}) collective-permute-start(f32[40,128]{1,0:T(8,128)S(1)} %max.18), channel_id=1, source_target_pairs={{0,2},{1,3},{2,0},{3,1},{4,6},{5,7},{6,4},{7,5},{8,10},{9,11},{10,... | collective-permute-start | bytes 61448 | tf_op jit(solution)/shard_map/ppermute | solution.py:323
  74.5 2.2 %collective-permute-done.17 = f32[40,128]{1,0:T(8,128)S(1)} collective-permute-done((f32[40,128]{1,0:T(8,128)S(1)}, f32[40,128]{1,0:T(8,128)S(1)}, u32[]{:S(2)}, u32[]{:S(2)}) %collective-permute-start.17) | collective-permute-done | bytes 20512 | tf_op jit(solution)/shard_map/ppermute | solution.py:323
  76.7 2.6 %collective-permute-start.18 = (f32[40,128]{1,0:T(8,128)S(1)}, f32[40,128]{1,0:T(8,128)S(1)}, u32[]{:S(2)}, u32[]{:S(2)}) collective-permute-start(f32[40,128]{1,0:T(8,128)S(1)} %max.19), channel_id=1, source_target_pairs={{0,4},{1,5},{2,6},{3,7},{4,0},{5,1},{6,2},{7,3},{8,12},{9,13},{10,... | collective-permute-start | bytes 61448 | tf_op jit(solution)/shard_map/ppermute | solution.py:323
  79.3 2.1 %collective-permute-done.18 = f32[40,128]{1,0:T(8,128)S(1)} collective-permute-done((f32[40,128]{1,0:T(8,128)S(1)}, f32[40,128]{1,0:T(8,128)S(1)}, u32[]{:S(2)}, u32[]{:S(2)}) %collective-permute-start.18) | collective-permute-done | bytes 20512 | tf_op jit(solution)/shard_map/ppermute | solution.py:323
  81.4 1.8 %collective-permute-start.21 = (f32[40,128]{1,0:T(8,128)S(1)}, f32[40,128]{1,0:T(8,128)S(1)}, u32[]{:S(2)}, u32[]{:S(2)}) collective-permute-start(f32[40,128]{1,0:T(8,128)S(1)} %max.20), channel_id=1, source_target_pairs={{0,24},{8,16},{16,8},{24,0},{1,25},{9,17},{17,9},{25,1},{2,26},{10... | collective-permute-start | bytes 61448 | tf_op jit(solution)/shard_map/ppermute | solution.py:323
  83.1 2.9 %collective-permute-done.21 = f32[40,128]{1,0:T(8,128)S(1)} collective-permute-done((f32[40,128]{1,0:T(8,128)S(1)}, f32[40,128]{1,0:T(8,128)S(1)}, u32[]{:S(2)}, u32[]{:S(2)}) %collective-permute-start.21) | collective-permute-done | bytes 20512 | tf_op jit(solution)/shard_map/ppermute | solution.py:323
  86.9 2.9 %collective-permute-done.20 = f32[40,128]{1,0:T(8,128)S(1)} collective-permute-done((f32[40,128]{1,0:T(8,128)S(1)}, f32[40,128]{1,0:T(8,128)S(1)}, u32[]{:S(2)}, u32[]{:S(2)}) %collective-permute-start.20) | collective-permute-done | bytes 20512 | tf_op jit(solution)/shard_map/ppermute | solution.py:323
  90.7 3.2 %collective-permute-done.19 = f32[40,128]{1,0:T(8,128)S(1)} collective-permute-done((f32[40,128]{1,0:T(8,128)S(1)}, f32[40,128]{1,0:T(8,128)S(1)}, u32[]{:S(2)}, u32[]{:S(2)}) %collective-permute-start.19) | collective-permute-done | bytes 20512 | tf_op jit(solution)/shard_map/ppermute | solution.py:323
  94.7 1.5 %collective-permute-start.11 = (f32[20,8,256]{2,1,0:T(8,128)S(1)}, f32[20,8,256]{2,1,0:T(8,128)S(1)}, u32[]{:S(2)}, u32[]{:S(2)}) collective-permute-start(f32[20,8,256]{2,1,0:T(8,128)S(1)} %get-tuple-element.47), channel_id=1, source_target_pairs={{0,16},{8,24},{16,0},{24,8},{1,17},{9,25},{17,1},{25,9},{2,18},{10... | collective-permute-start | bytes 491528 | tf_op jit(solution)/shard_map/ppermute | solution.py:323
  98.2 1.5 %collective-permute-start.9 = (f32[20,8,256]{2,1,0:T(8,128)S(1)}, f32[20,8,256]{2,1,0:T(8,128)S(1)}, u32[]{:S(2)}, u32[]{:S(2)}) collective-permute-start(f32[20,8,256]{2,1,0:T(8,128)S(1)} %get-tuple-element.44), channel_id=1, source_target_pairs={{0,24},{8,16},{16,8},{24,0},{1,25},{9,17},{17,9},{25,1},{2,26},{10... | collective-permute-start | bytes 491528 | tf_op jit(solution)/shard_map/ppermute | solution.py:323
  103.4 2.5 %collective-permute-done.8.refs_2_ = f32[20,8,256]{2,1,0:T(8,128)S(1)} collective-permute-done((f32[20,8,256]{2,1,0:T(8,128)S(1)}, f32[20,8,256]{2,1,0:T(8,128)S(1)}, u32[]{:S(2)}, u32[]{:S(2)}) %collective-permute-start.8) | collective-permute-done | bytes 163872 | tf_op jit(solution)/shard_map/ppermute | solution.py:323
  (50 shorter events, 17.4 us)
Async XLA Ops:
  0.6 1.4 %copy-start = (s32[96,4096]{1,0:T(8,128)S(1)}, s32[96,4096]{1,0:T(8,128)}, u32[]{:S(2)}) copy-start(s32[96,4096]{1,0:T(8,128)} %bins.1) | copy-start | bytes 4718596
  2.0 0.9 copy-start.1
  5.3 10.2 %collective-permute-start = (f32[16,4096]{1,0:T(8,128)S(1)}, f32[16,4096]{1,0:T(8,128)S(1)}, u32[]{:S(2)}, u32[]{:S(2)}) collective-permute-start(f32[16,4096]{1,0:T(8,128)S(1)} %get-tuple-element.33), channel_id=1, source_target_pairs={{0,8},{8,0},{16,24},{24,16},{1,9},{9,1},{17,25},{25,17},{2,10},{10... | collective-permute-start | bytes 786440 | tf_op jit(solution)/shard_map/ppermute | solution.py:323
  8.3 13.4 %collective-permute-start.1 = (f32[16,4096]{1,0:T(8,128)S(1)}, f32[16,4096]{1,0:T(8,128)S(1)}, u32[]{:S(2)}, u32[]{:S(2)}) collective-permute-start(f32[16,4096]{1,0:T(8,128)S(1)} %get-tuple-element.34), channel_id=1, source_target_pairs={{0,16},{8,24},{16,0},{24,8},{1,17},{9,25},{17,1},{25,9},{2,18},{10... | collective-permute-start | bytes 786440 | tf_op jit(solution)/shard_map/ppermute | solution.py:323
  9.8 11.9 %collective-permute-start.2 = (f32[16,4096]{1,0:T(8,128)S(1)}, f32[16,4096]{1,0:T(8,128)S(1)}, u32[]{:S(2)}, u32[]{:S(2)}) collective-permute-start(f32[16,4096]{1,0:T(8,128)S(1)} %get-tuple-element.35), channel_id=1, source_target_pairs={{0,24},{8,16},{16,8},{24,0},{1,25},{9,17},{17,9},{25,1},{2,26},{10... | collective-permute-start | bytes 786440 | tf_op jit(solution)/shard_map/ppermute | solution.py:323
  21.8 14.0 %collective-permute-start.3 = (f32[24,4096]{1,0:T(8,128)S(1)}, f32[24,4096]{1,0:T(8,128)S(1)}, u32[]{:S(2)}, u32[]{:S(2)}) collective-permute-start(f32[24,4096]{1,0:T(8,128)S(1)} %pad_maximum_fusion), channel_id=1, source_target_pairs={{0,1},{1,0},{2,3},{3,2},{4,5},{5,4},{6,7},{7,6},{8,9},{9,8},{10,11... | collective-permute-start | bytes 1179656 | tf_op jit(solution)/shard_map/ppermute | solution.py:323
  21.9 24.8 %collective-permute-start.4 = (f32[16,4096]{1,0:T(8,128)S(1)}, f32[16,4096]{1,0:T(8,128)S(1)}, u32[]{:S(2)}, u32[]{:S(2)}) collective-permute-start(f32[16,4096]{1,0:T(8,128)S(1)} %get-tuple-element.37), channel_id=1, source_target_pairs={{0,8},{8,0},{16,24},{24,16},{1,9},{9,1},{17,25},{25,17},{2,10},{10... | collective-permute-start | bytes 786440 | tf_op jit(solution)/shard_map/ppermute | solution.py:323
  23.1 23.6 %collective-permute-start.5 = (f32[16,4096]{1,0:T(8,128)S(1)}, f32[16,4096]{1,0:T(8,128)S(1)}, u32[]{:S(2)}, u32[]{:S(2)}) collective-permute-start(f32[16,4096]{1,0:T(8,128)S(1)} %get-tuple-element.38), channel_id=1, source_target_pairs={{0,16},{8,24},{16,0},{24,8},{1,17},{9,25},{17,1},{25,9},{2,18},{10... | collective-permute-start | bytes 786440 | tf_op jit(solution)/shard_map/ppermute | solution.py:323
  24.0 22.7 %collective-permute-start.6 = (f32[16,4096]{1,0:T(8,128)S(1)}, f32[16,4096]{1,0:T(8,128)S(1)}, u32[]{:S(2)}, u32[]{:S(2)}) collective-permute-start(f32[16,4096]{1,0:T(8,128)S(1)} %get-tuple-element.39), channel_id=1, source_target_pairs={{0,24},{8,16},{16,8},{24,0},{1,25},{9,17},{17,9},{25,1},{2,26},{10... | collective-permute-start | bytes 786440 | tf_op jit(solution)/shard_map/ppermute | solution.py:323
  56.8 37.9 %collective-permute-start.10 = (f32[20,8,256]{2,1,0:T(8,128)S(1)}, f32[20,8,256]{2,1,0:T(8,128)S(1)}, u32[]{:S(2)}, u32[]{:S(2)}) collective-permute-start(f32[20,8,256]{2,1,0:T(8,128)S(1)} %get-tuple-element.46), channel_id=1, source_target_pairs={{0,8},{8,0},{16,24},{24,16},{1,9},{9,1},{17,25},{25,17},{2,10},{10... | collective-permute-start | bytes 491528 | tf_op jit(solution)/shard_map/ppermute | solution.py:323
  58.0 38.1 %collective-permute-start.13 = (f32[20,8,256]{2,1,0:T(8,128)S(1)}, f32[20,8,256]{2,1,0:T(8,128)S(1)}, u32[]{:S(2)}, u32[]{:S(2)}) collective-permute-start(f32[20,8,256]{2,1,0:T(8,128)S(1)} %get-tuple-element.50), channel_id=1, source_target_pairs={{0,8},{8,0},{16,24},{24,16},{1,9},{9,1},{17,25},{25,17},{2,10},{10... | collective-permute-start | bytes 491528 | tf_op jit(solution)/shard_map/ppermute | solution.py:323
  58.9 38.4 %collective-permute-start.14 = (f32[20,8,256]{2,1,0:T(8,128)S(1)}, f32[20,8,256]{2,1,0:T(8,128)S(1)}, u32[]{:S(2)}, u32[]{:S(2)}) collective-permute-start(f32[20,8,256]{2,1,0:T(8,128)S(1)} %get-tuple-element.51), channel_id=1, source_target_pairs={{0,16},{8,24},{16,0},{24,8},{1,17},{9,25},{17,1},{25,9},{2,18},{10... | collective-permute-start | bytes 491528 | tf_op jit(solution)/shard_map/ppermute | solution.py:323
  60.4 37.8 %collective-permute-start.15 = (f32[20,8,256]{2,1,0:T(8,128)S(1)}, f32[20,8,256]{2,1,0:T(8,128)S(1)}, u32[]{:S(2)}, u32[]{:S(2)}) collective-permute-start(f32[20,8,256]{2,1,0:T(8,128)S(1)} %get-tuple-element.52), channel_id=1, source_target_pairs={{0,24},{8,16},{16,8},{24,0},{1,25},{9,17},{17,9},{25,1},{2,26},{10... | collective-permute-start | bytes 491528 | tf_op jit(solution)/shard_map/ppermute | solution.py:323
  71.6 1.3 %collective-permute-start.16 = (f32[40,128]{1,0:T(8,128)S(1)}, f32[40,128]{1,0:T(8,128)S(1)}, u32[]{:S(2)}, u32[]{:S(2)}) collective-permute-start(f32[40,128]{1,0:T(8,128)S(1)} %get-tuple-element.53), channel_id=1, source_target_pairs={{0,1},{1,0},{2,3},{3,2},{4,5},{5,4},{6,7},{7,6},{8,9},{9,8},{10,11... | collective-permute-start | bytes 61448 | tf_op jit(solution)/shard_map/ppermute | solution.py:323
  72.9 3.8 %collective-permute-start.17 = (f32[40,128]{1,0:T(8,128)S(1)}, f32[40,128]{1,0:T(8,128)S(1)}, u32[]{:S(2)}, u32[]{:S(2)}) collective-permute-start(f32[40,128]{1,0:T(8,128)S(1)} %max.18), channel_id=1, source_target_pairs={{0,2},{1,3},{2,0},{3,1},{4,6},{5,7},{6,4},{7,5},{8,10},{9,11},{10,... | collective-permute-start | bytes 61448 | tf_op jit(solution)/shard_map/ppermute | solution.py:323
  76.7 4.7 %collective-permute-start.18 = (f32[40,128]{1,0:T(8,128)S(1)}, f32[40,128]{1,0:T(8,128)S(1)}, u32[]{:S(2)}, u32[]{:S(2)}) collective-permute-start(f32[40,128]{1,0:T(8,128)S(1)} %max.19), channel_id=1, source_target_pairs={{0,4},{1,5},{2,6},{3,7},{4,0},{5,1},{6,2},{7,3},{8,12},{9,13},{10,... | collective-permute-start | bytes 61448 | tf_op jit(solution)/shard_map/ppermute | solution.py:323
  81.4 4.7 %collective-permute-start.21 = (f32[40,128]{1,0:T(8,128)S(1)}, f32[40,128]{1,0:T(8,128)S(1)}, u32[]{:S(2)}, u32[]{:S(2)}) collective-permute-start(f32[40,128]{1,0:T(8,128)S(1)} %max.20), channel_id=1, source_target_pairs={{0,24},{8,16},{16,8},{24,0},{1,25},{9,17},{17,9},{25,1},{2,26},{10... | collective-permute-start | bytes 61448 | tf_op jit(solution)/shard_map/ppermute | solution.py:323
  86.0 3.8 %collective-permute-start.20 = (f32[40,128]{1,0:T(8,128)S(1)}, f32[40,128]{1,0:T(8,128)S(1)}, u32[]{:S(2)}, u32[]{:S(2)}) collective-permute-start(f32[40,128]{1,0:T(8,128)S(1)} %max.20), channel_id=1, source_target_pairs={{0,16},{8,24},{16,0},{24,8},{1,17},{9,25},{17,1},{25,9},{2,18},{10... | collective-permute-start | bytes 61448 | tf_op jit(solution)/shard_map/ppermute | solution.py:323
  89.8 4.0 %collective-permute-start.19 = (f32[40,128]{1,0:T(8,128)S(1)}, f32[40,128]{1,0:T(8,128)S(1)}, u32[]{:S(2)}, u32[]{:S(2)}) collective-permute-start(f32[40,128]{1,0:T(8,128)S(1)} %max.20), channel_id=1, source_target_pairs={{0,8},{8,0},{16,24},{24,16},{1,9},{9,1},{17,25},{25,17},{2,10},{10... | collective-permute-start | bytes 61448 | tf_op jit(solution)/shard_map/ppermute | solution.py:323
  93.8 9.5 %collective-permute-start.7 = (f32[20,8,256]{2,1,0:T(8,128)S(1)}, f32[20,8,256]{2,1,0:T(8,128)S(1)}, u32[]{:S(2)}, u32[]{:S(2)}) collective-permute-start(f32[20,8,256]{2,1,0:T(8,128)S(1)} %get-tuple-element.42), channel_id=1, source_target_pairs={{0,8},{8,0},{16,24},{24,16},{1,9},{9,1},{17,25},{25,17},{2,10},{10... | collective-permute-start | bytes 491528 | tf_op jit(solution)/shard_map/ppermute | solution.py:323
  94.7 6.7 %collective-permute-start.11 = (f32[20,8,256]{2,1,0:T(8,128)S(1)}, f32[20,8,256]{2,1,0:T(8,128)S(1)}, u32[]{:S(2)}, u32[]{:S(2)}) collective-permute-start(f32[20,8,256]{2,1,0:T(8,128)S(1)} %get-tuple-element.47), channel_id=1, source_target_pairs={{0,16},{8,24},{16,0},{24,8},{1,17},{9,25},{17,1},{25,9},{2,18},{10... | collective-permute-start | bytes 491528 | tf_op jit(solution)/shard_map/ppermute | solution.py:323
  96.2 6.3 %collective-permute-start.12 = (f32[20,8,256]{2,1,0:T(8,128)S(1)}, f32[20,8,256]{2,1,0:T(8,128)S(1)}, u32[]{:S(2)}, u32[]{:S(2)}) collective-permute-start(f32[20,8,256]{2,1,0:T(8,128)S(1)} %get-tuple-element.48), channel_id=1, source_target_pairs={{0,24},{8,16},{16,8},{24,0},{1,25},{9,17},{17,9},{25,1},{2,26},{10... | collective-permute-start | bytes 491528 | tf_op jit(solution)/shard_map/ppermute | solution.py:323
  97.3 8.6 %collective-permute-start.8 = (f32[20,8,256]{2,1,0:T(8,128)S(1)}, f32[20,8,256]{2,1,0:T(8,128)S(1)}, u32[]{:S(2)}, u32[]{:S(2)}) collective-permute-start(f32[20,8,256]{2,1,0:T(8,128)S(1)} %get-tuple-element.43), channel_id=1, source_target_pairs={{0,16},{8,24},{16,0},{24,8},{1,17},{9,25},{17,1},{25,9},{2,18},{10... | collective-permute-start | bytes 491528 | tf_op jit(solution)/shard_map/ppermute | solution.py:323
  98.2 7.7 %collective-permute-start.9 = (f32[20,8,256]{2,1,0:T(8,128)S(1)}, f32[20,8,256]{2,1,0:T(8,128)S(1)}, u32[]{:S(2)}, u32[]{:S(2)}) collective-permute-start(f32[20,8,256]{2,1,0:T(8,128)S(1)} %get-tuple-element.44), channel_id=1, source_target_pairs={{0,24},{8,16},{16,8},{24,0},{1,25},{9,17},{17,9},{25,1},{2,26},{10... | collective-permute-start | bytes 491528 | tf_op jit(solution)/shard_map/ppermute | solution.py:323
  (3 other events, 2.1 us)

commit v2 on v1

--- a/solution.py
+++ b/solution.py
@@ -75,16 +75,27 @@
             turn += 1
 
 
-def prepare_kernel(group, owned, size, me, parity, bins, nodes, fold, gradient, hessian, *refs):
+def prepare_kernel(group, owned, size, me, parity, *refs):
+    distant, refs = refs[:5], refs[5:]
+    near, sems = refs[-6:-1], refs[-1]
+    copies = [pltpu.make_async_copy(a, b, sems.at[i]) for i, (a, b) in enumerate(zip(distant, near))]
+    for copy in copies:
+        copy.start()
+    bins, nodes, fold, gradient, hessian = near
+    refs = refs[:-6]
     first, later = refs[: group - 1], refs[group - 1 : -2]
     own, rowdata = refs[-2:]
     rows = bins.shape[1]
+    for copy in copies[1:]:
+        copy.wait()
     rowdata[0:FOLDS] = nodes[...].astype(F32)
     rowdata[FOLDS + 3 :] = jnp.zeros((16 - FOLDS - 3, rows), F32)
     for i, ref in enumerate((fold, gradient, hessian)):
         lines = ref[...].astype(F32)
         for j in range(rows // 128):
             rowdata[FOLDS + i : FOLDS + i + 1, j * 128 : j * 128 + 128] = lines[j : j + 1]
+
+    copies[0].wait()
 
     def move(to, at, source, count):
         if owned % 8 == 0:
@@ -109,15 +120,18 @@
         shapes += [(owned - size, rows)] * (group - 1)
     shapes += [(owned, rows), (16, rows)]
     wide = (rows // 128, 128)
+    given = (bins, nodes.T, fold.reshape(wide), gradient.reshape(wide), hessian.reshape(wide))
     out = pl.pallas_call(
         functools.partial(prepare_kernel, group, owned, size),
         out_shape=[jax.ShapeDtypeStruct(shape, F32) for shape in shapes],
-        in_specs=[SMEM, SMEM] + [VMEM] * 5,
+        in_specs=[SMEM, SMEM] + [pl.BlockSpec(memory_space=pltpu.HBM)] * 5,
         out_specs=[VMEM] * len(shapes),
+        scratch_shapes=[pltpu.VMEM(x.shape, x.dtype) for x in given]
+        + [pltpu.SemaphoreType.DMA((5,))],
         compiler_params=params(),
         cost_estimate=cost(1 << 30),
         name="prepare",
-    )(me, parity, bins, nodes.T, fold.reshape(wide), gradient.reshape(wide), hessian.reshape(wide))
+    )(me, parity, *given)
     return out[: group - 1], out[group - 1 : -2], out[-2], out[-1]
 
 
@@ -144,7 +158,7 @@
                     out[at] = pltpu.matmul_pop(acc)
                 return carry
 
-            lax.fori_loop(0, size // 2, visit, 0)
+            lax.fori_loop(0, size // 2, visit, 0, unroll=2 if size % 4 == 0 else 1)
 
     pl.run_scoped(body, pltpu.ACC(0)((COLS, BINS), F32), pltpu.ACC(1)((COLS, BINS), F32))
 
@@ -194,14 +208,11 @@
     )(parity, *mine, other)
 
 
-def chunk_kernel(count, group, line, feats, rows, final, me, part, best_in, weights, *refs):
-    bins, pieces, best_out, held = refs[:count], refs[count:-2], refs[-2], refs[-1]
+def chunk_kernel(count, group, line, feats, rows, final, waiting, me, part, best_in, weights, *refs):
+    bins, ready, refs = refs[:count], refs[count : count + waiting], refs[count + waiting :]
     levels = bin_levels()
-    lower = lax.broadcasted_iota(jnp.int32, (BINS, BINS), 0)
-    upper = lax.broadcasted_iota(jnp.int32, (BINS, BINS), 1)
-    triangle = (lower <= upper).astype(BF16)
-    last = lax.broadcasted_iota(jnp.int32, (PAIRS, BINS), 1) == BINS - 1
     sources = [(bins[s], line, weights, s * rows, rows) for s in range(count)]
+    held = refs[-1]
 
     def body(acc0, acc1):
         accs = (acc0, acc1)
@@ -216,15 +227,21 @@
             return carry
 
         lax.fori_loop(0, feats // 2, visit, 0)
-
+        if not group:
+            return
+        lower = lax.broadcasted_iota(jnp.int32, (BINS, BINS), 0)
+        upper = lax.broadcasted_iota(jnp.int32, (BINS, BINS), 1)
+        triangle = (lower <= upper).astype(BF16)
+        last = lax.broadcasted_iota(jnp.int32, (PAIRS, BINS), 1) == BINS - 1
         best = best_in[...]
-        for p in range(feats // 2):
+        lists = [(ref, f) for ref in (*ready, held) for f in range(feats)]
+        for p in range(0, len(lists), 2):
             for q, acc in enumerate(accs):
-                f = 2 * p + q
+                ref, f = lists[p + q]
                 if p == 0:
                     pltpu.matmul_push_rhs(triangle, staging_register=0, mxu_index=q)
                 at = slice(f * COLS, (f + 1) * COLS)
-                rest = jnp.concatenate([held[0, at], held[1, at]], axis=1)
+                rest = jnp.concatenate([ref[0, at], ref[1, at]], axis=1)
                 for piece in range(3):
                     high = rest.astype(BF16)
                     rest = rest - high.astype(F32)
@@ -243,36 +260,43 @@
                 best = jnp.maximum(best, jnp.where(last, F32(-3e38), gain))
         if final:
             best = jnp.broadcast_to(jnp.max(best, axis=1, keepdims=True), (PAIRS, 128))
-        best_out[...] = best
+        refs[group][...] = best
 
     pl.run_scoped(body, pltpu.ACC(0)((COLS, BINS), F32), pltpu.ACC(1)((COLS, BINS), F32))
 
-    share = COLS // group
     for d in range(group):
+        share = COLS // group
         for j in range(share):
             row = (j % 2) * PAIRS + (me[0] ^ d) * (share // 2) + j // 2
             for half in range(2):
-                pieces[d][j, :, half * 128 : half * 128 + 128] = held[
-                    half, pl.ds(row, feats, stride=COLS), :
-                ]
-
-
-def chunk(me, part, best, weights, bins, line, feats, group, final):
+                lanes = slice(half * 128, half * 128 + 128)
+                for c, ref in enumerate((*ready, held)):
+                    refs[d][j, c * feats : (c + 1) * feats, lanes] = ref[
+                        half, pl.ds(row, feats, stride=COLS), :
+                    ]
+
+
+def chunk(me, part, best, weights, bins, line, feats, group, final, ready):
     count = len(bins)
     rows = weights.shape[1] // count
-    share = COLS // group
-    piece = jax.ShapeDtypeStruct((share, feats, BINS), F32)
+    held = (2, feats * COLS, 128)
+    if group:
+        piece = (COLS // group, feats * (len(ready) + 1), BINS)
+        shapes = [piece] * group + [(PAIRS, 128 if final else BINS)]
+        scratch = [pltpu.VMEM(held, F32)]
+    else:
+        shapes, scratch = [held], []
     out = pl.pallas_call(
-        functools.partial(chunk_kernel, count, group, line, feats, rows, final),
-        out_shape=[piece] * group + [jax.ShapeDtypeStruct((PAIRS, 128 if final else BINS), F32)],
-        in_specs=[SMEM, VMEM, VMEM, VMEM] + [VMEM] * count,
-        out_specs=[VMEM] * (group + 1),
-        scratch_shapes=[pltpu.VMEM((2, feats * COLS, 128), F32)],
+        functools.partial(chunk_kernel, count, group, line, feats, rows, final, len(ready)),
+        out_shape=[jax.ShapeDtypeStruct(shape, F32) for shape in shapes],
+        in_specs=[SMEM, VMEM, VMEM, VMEM] + [VMEM] * (count + len(ready)),
+        out_specs=[VMEM] * len(shapes),
+        scratch_shapes=scratch,
         compiler_params=params(),
         cost_estimate=cost(2 * feats * rows * count * COLS * BINS),
         name="chunk",
-    )(me, part, best, weights, *bins)
-    return out[:-1], out[-1]
+    )(me, part, best, weights, *bins, *ready)
+    return out
 
 
 def place_kernel(group, first, owned, feats, me, *refs):
@@ -332,22 +356,27 @@
     traded = swap(jnp.concatenate([a[:8] for a in arrived]), "feat", feat_size, 1)
     weights = remote_weights(parity, arrived, traded)
     best = jnp.full((PAIRS, BINS), -3e38, F32)
-    received = []
+    received, ready, began = [], [], 0
     for c in range(chunks):
         left = chunks - 1 - c
+        send = left == 0 or left == 1
         source, line = (arrived, 8) if c == 0 else (later, (c - 1) * size)
-        pieces, best = chunk(
-            me, part[c], best, weights, source, line, size, group, left == 0
-        )
-        received.append([pieces[0]] + [swap(pieces[d], "rows", group, d) for d in others])
+        made = chunk(me, part[c], best, weights, source, line, size, group * send, left == 0, ready)
+        if not send:
+            ready = ready + list(made)
+            continue
+        best = made[-1]
+        sent = [swap(made[d], "rows", group, d) for d in others]
+        received.append((left, began, [made[0]] + sent))
+        ready, began = [], (c + 1) * size
     step = 1
     while step < feat_size:
         best = jnp.maximum(best, swap(best, "feat", feat_size, step))
         step *= 2
     tops = [swap(best, "rows", group, d) for d in others]
     out = None
-    for c, pieces in enumerate(received):
-        out = place(me, out, pieces, c * size, owned, (COLS // group, feats, BINS))
+    for left, at, pieces in received:
+        out = place(me, out, pieces, at, owned, (COLS // group, feats, BINS))
     for top in tops:
         best = jnp.maximum(best, top)
     return out, best[:, 0].reshape(FOLDS, NODES)

time: 107 us -> 97.3 us (0.909)
  waiting for transfers between devices: 30 us -> 24.3 us
  starting transfers between devices: 26.4 us -> 23.4 us
  Pallas kernels: 44.1 us -> 43 us
    ppermute x22 -> x19, waiting for transfers between devices: 30 us -> 24.3 us  [swap(): return lax.ppermute(x, axis, [(i, i ^ d) for i in range(count)])]
    ppermute x22 -> x19, starting transfers between devices: 26.4 us -> 23.4 us  [swap(): return lax.ppermute(x, axis, [(i, i ^ d) for i in range(count)])]
    pallas_call x3 -> x2, Pallas kernels: 2.59 us -> 1.94 us  [place(): pl.pallas_call(functools.partial(place_kernel, group, first, owned, feats...]
  transfers between devices with their start and end apart: 22 -> 19, of which waited for: 10 -> 9; matrix products, arithmetic and copies ran while one was open for 1% -> 1% of each run, Pallas kernels for 31% -> 32%
where the time goes in v2:
time: 97.3 us; the launch traced here: 97 us
  Pallas kernels  43 us (44%)
  waiting for transfers between devices  24.3 us (25%)
  starting transfers between devices  23.4 us (24%)
  local copies, waits for them, and re-layouts  5.25 us (5%)
    pallas_call x3, Pallas kernels, chunk(): pl.pallas_call(functools.partial(chunk_kernel, count, group, line, feats,...  30.1 us
    ppermute x19, waiting for transfers between devices, swap(): return lax.ppermute(x, axis, [(i, i ^ d) for i in range(count)])  24.3 us
    ppermute x19, starting transfers between devices, swap(): return lax.ppermute(x, axis, [(i, i ^ d) for i in range(count)])  23.4 us
    pallas_call x1, Pallas kernels, own_part(): pl.pallas_call(own_kernel, out_shape=[out] * (feats // size), in_specs=[V...  9.71 us
    unnamed x11, local copies, waits for them, and re-layouts  5.14 us
  transfers between devices with their start and end apart: 19, of which 9 were waited for; matrix products, arithmetic and copies ran while one was open for 1% of the time, Pallas kernels for 32%

profile of v2, /device:TPU:0, one launch (start us, length us, event | category | flops | bytes accessed | tf_op | source)
XLA Modules:
  0.0 97.0 jit_solution(13314656499969306951)
XLA Ops:
  0.6 1.4 %copy-done = s32[96,4096]{1,0:T(8,128)S(1)} copy-done((s32[96,4096]{1,0:T(8,128)S(1)}, s32[96,4096]{1,0:T(8,128)}, u32[]{:S(2)}) %copy-start) | copy-done | bytes 1572888
  5.5 3.0 %collective-permute-start = (f32[16,4096]{1,0:T(8,128)S(1)}, f32[16,4096]{1,0:T(8,128)S(1)}, u32[]{:S(2)}, u32[]{:S(2)}) collective-permute-start(f32[16,4096]{1,0:T(8,128)S(1)} %get-tuple-element.27), channel_id=1, source_target_pairs={{0,8},{8,0},{16,24},{24,16},{1,9},{9,1},{17,25},{25,17},{2,10},{10... | collective-permute-start | bytes 786440 | tf_op jit(solution)/shard_map/ppermute | solution.py:347
  8.5 1.5 %collective-permute-start.1 = (f32[16,4096]{1,0:T(8,128)S(1)}, f32[16,4096]{1,0:T(8,128)S(1)}, u32[]{:S(2)}, u32[]{:S(2)}) collective-permute-start(f32[16,4096]{1,0:T(8,128)S(1)} %get-tuple-element.28), channel_id=1, source_target_pairs={{0,16},{8,24},{16,0},{24,8},{1,17},{9,25},{17,1},{25,9},{2,18},{10... | collective-permute-start | bytes 786440 | tf_op jit(solution)/shard_map/ppermute | solution.py:347
  10.1 5.6 %collective-permute-done.refs_0_ = f32[16,4096]{1,0:T(8,128)S(1)} collective-permute-done((f32[16,4096]{1,0:T(8,128)S(1)}, f32[16,4096]{1,0:T(8,128)S(1)}, u32[]{:S(2)}, u32[]{:S(2)}) %collective-permute-start) | collective-permute-done | bytes 262176 | tf_op jit(solution)/shard_map/ppermute | solution.py:347
  15.7 6.2 %collective-permute-done.1.refs_1_ = f32[16,4096]{1,0:T(8,128)S(1)} collective-permute-done((f32[16,4096]{1,0:T(8,128)S(1)}, f32[16,4096]{1,0:T(8,128)S(1)}, u32[]{:S(2)}, u32[]{:S(2)}) %collective-permute-start.1) | collective-permute-done | bytes 262176 | tf_op jit(solution)/shard_map/ppermute | solution.py:347
  22.1 1.3 %collective-permute-start.4 = (f32[16,4096]{1,0:T(8,128)S(1)}, f32[16,4096]{1,0:T(8,128)S(1)}, u32[]{:S(2)}, u32[]{:S(2)}) collective-permute-start(f32[16,4096]{1,0:T(8,128)S(1)} %get-tuple-element.30), channel_id=1, source_target_pairs={{0,8},{8,0},{16,24},{24,16},{1,9},{9,1},{17,25},{25,17},{2,10},{10... | collective-permute-start | bytes 786440 | tf_op jit(solution)/shard_map/ppermute | solution.py:347
  24.2 1.4 %collective-permute-start.6 = (f32[16,4096]{1,0:T(8,128)S(1)}, f32[16,4096]{1,0:T(8,128)S(1)}, u32[]{:S(2)}, u32[]{:S(2)}) collective-permute-start(f32[16,4096]{1,0:T(8,128)S(1)} %get-tuple-element.32), channel_id=1, source_target_pairs={{0,24},{8,16},{16,8},{24,0},{1,25},{9,17},{17,9},{25,1},{2,26},{10... | collective-permute-start | bytes 786440 | tf_op jit(solution)/shard_map/ppermute | solution.py:347
  25.6 9.7 %own_part.1 = (f32[640,256]{1,0:T(8,128)S(1)}, f32[640,256]{1,0:T(8,128)S(1)}, f32[640,256]{1,0:T(8,128)S(1)}) custom-call(f32[24,4096]{1,0:T(8,128)S(1)} %get-tuple-element.23.bins, f32[16,4096]{1,0:T(8,128)S(1)} %get-tuple-element.24.rowdata), custom_call_target="tpu_custom_call" | custom-call | flops 4026531840 | bytes 1048576 | tf_op jit(solution)/shard_map/own_part/pallas_call | solution.py:169
  36.2 9.1 %chunk.3.refs_3_ = f32[2,640,128]{2,1,0:T(8,128)S(1)} custom-call(s32[1]{0:T(128)} %bitcast.me, f32[640,256]{1,0:T(8,128)S(1)} %get-tuple-element.33.part, f32[40,256]{1,0:T(8,128)S(1)} %broadcast_in_dim.11.best_in, bf16[80,12288]{1,0:T(8,128)(2,1)S(1)} %remote_weights.1.weights, f32[16,4096]{1,0:T(8,128)S(1)} %collective-permute-done.refs_0_, ...), custom_call_target="tpu_custom_call" | custom-call | flops 4026531840 | bytes 1048576 | tf_op jit(solution)/shard_map/chunk/pallas_call | solution.py:289
  45.3 11.0 %chunk.4 = (f32[20,16,256]{2,1,0:T(8,128)S(1)}, f32[20,16,256]{2,1,0:T(8,128)S(1)}, f32[20,16,256]{2,1,0:T(8,128)S(1)}, f32[20,16,256]{2,1,0:T(8,128)S(1)}, f32[40,256]{1,0:T(8,128)S(1)}) custom-call(s32[1]{0:T(128)} %bitcast.me, f32[640,256]{1,0:T(8,128)S(1)} %get-tuple-element.26.part, f32[40,256]{1,0:T(8,128)S(1)} %broadcast_in_dim.11.best_in, ...), custom_call_target="tpu_custom_call" | custom-call | flops 4026531840 | bytes 1048576 | tf_op jit(solution)/shard_map/chunk/pallas_call | solution.py:289
  56.2 1.3 %collective-permute-start.10 = (f32[20,16,256]{2,1,0:T(8,128)S(1)}, f32[20,16,256]{2,1,0:T(8,128)S(1)}, u32[]{:S(2)}, u32[]{:S(2)}) collective-permute-start(f32[20,16,256]{2,1,0:T(8,128)S(1)} %get-tuple-element.40), channel_id=1, source_target_pairs={{0,8},{8,0},{16,24},{24,16},{1,9},{9,1},{17,25},{25,17},{2,10},{10... | collective-permute-start | bytes 983048 | tf_op jit(solution)/shard_map/ppermute | solution.py:347
  58.3 1.4 %collective-permute-start.12 = (f32[20,16,256]{2,1,0:T(8,128)S(1)}, f32[20,16,256]{2,1,0:T(8,128)S(1)}, u32[]{:S(2)}, u32[]{:S(2)}) collective-permute-start(f32[20,16,256]{2,1,0:T(8,128)S(1)} %get-tuple-element.42), channel_id=1, source_target_pairs={{0,24},{8,16},{16,8},{24,0},{1,25},{9,17},{17,9},{25,1},{2,26},{10... | collective-permute-start | bytes 983048 | tf_op jit(solution)/shard_map/ppermute | solution.py:347
  59.8 10.1 %chunk.5 = (f32[20,8,256]{2,1,0:T(8,128)S(1)}, f32[20,8,256]{2,1,0:T(8,128)S(1)}, f32[20,8,256]{2,1,0:T(8,128)S(1)}, f32[20,8,256]{2,1,0:T(8,128)S(1)}, f32[40,128]{1,0:T(8,128)S(1)}) custom-call(s32[1]{0:T(128)} %bitcast.me, f32[640,256]{1,0:T(8,128)S(1)} %get-tuple-element.25.part, f32[40,256]{1,0:T(8,128)S(1)} %get-tuple-element.34.best_in, ...), custom_call_target="tpu_custom_call" | custom-call | flops 4026531840 | bytes 1048576 | tf_op jit(solution)/shard_map/chunk/pallas_call | solution.py:289
  71.2 1.6 %collective-permute-start.14 = (f32[40,128]{1,0:T(8,128)S(1)}, f32[40,128]{1,0:T(8,128)S(1)}, u32[]{:S(2)}, u32[]{:S(2)}) collective-permute-start(f32[40,128]{1,0:T(8,128)S(1)} %max.18), channel_id=1, source_target_pairs={{0,2},{1,3},{2,0},{3,1},{4,6},{5,7},{6,4},{7,5},{8,10},{9,11},{10,... | collective-permute-start | bytes 61448 | tf_op jit(solution)/shard_map/ppermute | solution.py:347
  72.8 2.2 %collective-permute-done.14 = f32[40,128]{1,0:T(8,128)S(1)} collective-permute-done((f32[40,128]{1,0:T(8,128)S(1)}, f32[40,128]{1,0:T(8,128)S(1)}, u32[]{:S(2)}, u32[]{:S(2)}) %collective-permute-start.14) | collective-permute-done | bytes 20512 | tf_op jit(solution)/shard_map/ppermute | solution.py:347
  75.0 2.6 %collective-permute-start.15 = (f32[40,128]{1,0:T(8,128)S(1)}, f32[40,128]{1,0:T(8,128)S(1)}, u32[]{:S(2)}, u32[]{:S(2)}) collective-permute-start(f32[40,128]{1,0:T(8,128)S(1)} %max.19), channel_id=1, source_target_pairs={{0,4},{1,5},{2,6},{3,7},{4,0},{5,1},{6,2},{7,3},{8,12},{9,13},{10,... | collective-permute-start | bytes 61448 | tf_op jit(solution)/shard_map/ppermute | solution.py:347
  77.6 2.1 %collective-permute-done.15 = f32[40,128]{1,0:T(8,128)S(1)} collective-permute-done((f32[40,128]{1,0:T(8,128)S(1)}, f32[40,128]{1,0:T(8,128)S(1)}, u32[]{:S(2)}, u32[]{:S(2)}) %collective-permute-start.15) | collective-permute-done | bytes 20512 | tf_op jit(solution)/shard_map/ppermute | solution.py:347
  79.7 1.5 %collective-permute-start.18 = (f32[40,128]{1,0:T(8,128)S(1)}, f32[40,128]{1,0:T(8,128)S(1)}, u32[]{:S(2)}, u32[]{:S(2)}) collective-permute-start(f32[40,128]{1,0:T(8,128)S(1)} %max.20), channel_id=1, source_target_pairs={{0,24},{8,16},{16,8},{24,0},{1,25},{9,17},{17,9},{25,1},{2,26},{10... | collective-permute-start | bytes 61448 | tf_op jit(solution)/shard_map/ppermute | solution.py:347
  82.3 2.0 %collective-permute-done.18 = f32[40,128]{1,0:T(8,128)S(1)} collective-permute-done((f32[40,128]{1,0:T(8,128)S(1)}, f32[40,128]{1,0:T(8,128)S(1)}, u32[]{:S(2)}, u32[]{:S(2)}) %collective-permute-start.18) | collective-permute-done | bytes 20512 | tf_op jit(solution)/shard_map/ppermute | solution.py:347
  84.3 1.2 %collective-permute-start.16 = (f32[40,128]{1,0:T(8,128)S(1)}, f32[40,128]{1,0:T(8,128)S(1)}, u32[]{:S(2)}, u32[]{:S(2)}) collective-permute-start(f32[40,128]{1,0:T(8,128)S(1)} %max.20), channel_id=1, source_target_pairs={{0,8},{8,0},{16,24},{24,16},{1,9},{9,1},{17,25},{25,17},{2,10},{10... | collective-permute-start | bytes 61448 | tf_op jit(solution)/shard_map/ppermute | solution.py:347
  86.4 1.9 %collective-permute-done.16 = f32[40,128]{1,0:T(8,128)S(1)} collective-permute-done((f32[40,128]{1,0:T(8,128)S(1)}, f32[40,128]{1,0:T(8,128)S(1)}, u32[]{:S(2)}, u32[]{:S(2)}) %collective-permute-start.16) | collective-permute-done | bytes 20512 | tf_op jit(solution)/shard_map/ppermute | solution.py:347
  88.3 1.5 %collective-permute-start.8 = (f32[20,8,256]{2,1,0:T(8,128)S(1)}, f32[20,8,256]{2,1,0:T(8,128)S(1)}, u32[]{:S(2)}, u32[]{:S(2)}) collective-permute-start(f32[20,8,256]{2,1,0:T(8,128)S(1)} %get-tuple-element.37), channel_id=1, source_target_pairs={{0,16},{8,24},{16,0},{24,8},{1,17},{9,25},{17,1},{25,9},{2,18},{10... | collective-permute-start | bytes 491528 | tf_op jit(solution)/shard_map/ppermute | solution.py:347
  93.0 1.5 %collective-permute-done.8.refs_2_ = f32[20,8,256]{2,1,0:T(8,128)S(1)} collective-permute-done((f32[20,8,256]{2,1,0:T(8,128)S(1)}, f32[20,8,256]{2,1,0:T(8,128)S(1)}, u32[]{:S(2)}, u32[]{:S(2)}) %collective-permute-start.8) | collective-permute-done | bytes 163872 | tf_op jit(solution)/shard_map/ppermute | solution.py:347
  94.5 1.6 %collective-permute-done.9.refs_3_ = f32[20,8,256]{2,1,0:T(8,128)S(1)} collective-permute-done((f32[20,8,256]{2,1,0:T(8,128)S(1)}, f32[20,8,256]{2,1,0:T(8,128)S(1)}, u32[]{:S(2)}, u32[]{:S(2)}) %collective-permute-start.9) | collective-permute-done | bytes 163872 | tf_op jit(solution)/shard_map/ppermute | solution.py:347
  (43 shorter events, 13.4 us)
Async XLA Ops:
  0.6 1.4 %copy-start = (s32[96,4096]{1,0:T(8,128)S(1)}, s32[96,4096]{1,0:T(8,128)}, u32[]{:S(2)}) copy-start(s32[96,4096]{1,0:T(8,128)} %refs_0_.1) | copy-start | bytes 4718596
  2.0 0.9 copy-start.1
  3.0 0.7 copy-start.2
  3.7 0.7 copy-start.3
  4.4 0.7 copy-start.4
  5.5 10.2 %collective-permute-start = (f32[16,4096]{1,0:T(8,128)S(1)}, f32[16,4096]{1,0:T(8,128)S(1)}, u32[]{:S(2)}, u32[]{:S(2)}) collective-permute-start(f32[16,4096]{1,0:T(8,128)S(1)} %get-tuple-element.27), channel_id=1, source_target_pairs={{0,8},{8,0},{16,24},{24,16},{1,9},{9,1},{17,25},{25,17},{2,10},{10... | collective-permute-start | bytes 786440 | tf_op jit(solution)/shard_map/ppermute | solution.py:347
  8.5 13.4 %collective-permute-start.1 = (f32[16,4096]{1,0:T(8,128)S(1)}, f32[16,4096]{1,0:T(8,128)S(1)}, u32[]{:S(2)}, u32[]{:S(2)}) collective-permute-start(f32[16,4096]{1,0:T(8,128)S(1)} %get-tuple-element.28), channel_id=1, source_target_pairs={{0,16},{8,24},{16,0},{24,8},{1,17},{9,25},{17,1},{25,9},{2,18},{10... | collective-permute-start | bytes 786440 | tf_op jit(solution)/shard_map/ppermute | solution.py:347
  10.1 11.9 %collective-permute-start.2 = (f32[16,4096]{1,0:T(8,128)S(1)}, f32[16,4096]{1,0:T(8,128)S(1)}, u32[]{:S(2)}, u32[]{:S(2)}) collective-permute-start(f32[16,4096]{1,0:T(8,128)S(1)} %get-tuple-element.29), channel_id=1, source_target_pairs={{0,24},{8,16},{16,8},{24,0},{1,25},{9,17},{17,9},{25,1},{2,26},{10... | collective-permute-start | bytes 786440 | tf_op jit(solution)/shard_map/ppermute | solution.py:347
  22.0 13.3 %collective-permute-start.3 = (f32[24,4096]{1,0:T(8,128)S(1)}, f32[24,4096]{1,0:T(8,128)S(1)}, u32[]{:S(2)}, u32[]{:S(2)}) collective-permute-start(f32[24,4096]{1,0:T(8,128)S(1)} %pad_maximum_fusion), channel_id=1, source_target_pairs={{0,1},{1,0},{2,3},{3,2},{4,5},{5,4},{6,7},{7,6},{8,9},{9,8},{10,11... | collective-permute-start | bytes 1179656 | tf_op jit(solution)/shard_map/ppermute | solution.py:347
  22.1 23.1 %collective-permute-start.4 = (f32[16,4096]{1,0:T(8,128)S(1)}, f32[16,4096]{1,0:T(8,128)S(1)}, u32[]{:S(2)}, u32[]{:S(2)}) collective-permute-start(f32[16,4096]{1,0:T(8,128)S(1)} %get-tuple-element.30), channel_id=1, source_target_pairs={{0,8},{8,0},{16,24},{24,16},{1,9},{9,1},{17,25},{25,17},{2,10},{10... | collective-permute-start | bytes 786440 | tf_op jit(solution)/shard_map/ppermute | solution.py:347
  23.4 21.9 %collective-permute-start.5 = (f32[16,4096]{1,0:T(8,128)S(1)}, f32[16,4096]{1,0:T(8,128)S(1)}, u32[]{:S(2)}, u32[]{:S(2)}) collective-permute-start(f32[16,4096]{1,0:T(8,128)S(1)} %get-tuple-element.31), channel_id=1, source_target_pairs={{0,16},{8,24},{16,0},{24,8},{1,17},{9,25},{17,1},{25,9},{2,18},{10... | collective-permute-start | bytes 786440 | tf_op jit(solution)/shard_map/ppermute | solution.py:347
  24.2 21.0 %collective-permute-start.6 = (f32[16,4096]{1,0:T(8,128)S(1)}, f32[16,4096]{1,0:T(8,128)S(1)}, u32[]{:S(2)}, u32[]{:S(2)}) collective-permute-start(f32[16,4096]{1,0:T(8,128)S(1)} %get-tuple-element.32), channel_id=1, source_target_pairs={{0,24},{8,16},{16,8},{24,0},{1,25},{9,17},{17,9},{25,1},{2,26},{10... | collective-permute-start | bytes 786440 | tf_op jit(solution)/shard_map/ppermute | solution.py:347
  56.2 33.6 %collective-permute-start.10 = (f32[20,16,256]{2,1,0:T(8,128)S(1)}, f32[20,16,256]{2,1,0:T(8,128)S(1)}, u32[]{:S(2)}, u32[]{:S(2)}) collective-permute-start(f32[20,16,256]{2,1,0:T(8,128)S(1)} %get-tuple-element.40), channel_id=1, source_target_pairs={{0,8},{8,0},{16,24},{24,16},{1,9},{9,1},{17,25},{25,17},{2,10},{10... | collective-permute-start | bytes 983048 | tf_op jit(solution)/shard_map/ppermute | solution.py:347
  57.5 34.4 %collective-permute-start.11 = (f32[20,16,256]{2,1,0:T(8,128)S(1)}, f32[20,16,256]{2,1,0:T(8,128)S(1)}, u32[]{:S(2)}, u32[]{:S(2)}) collective-permute-start(f32[20,16,256]{2,1,0:T(8,128)S(1)} %get-tuple-element.41), channel_id=1, source_target_pairs={{0,16},{8,24},{16,0},{24,8},{1,17},{9,25},{17,1},{25,9},{2,18},{10... | collective-permute-start | bytes 983048 | tf_op jit(solution)/shard_map/ppermute | solution.py:347
  58.3 33.6 %collective-permute-start.12 = (f32[20,16,256]{2,1,0:T(8,128)S(1)}, f32[20,16,256]{2,1,0:T(8,128)S(1)}, u32[]{:S(2)}, u32[]{:S(2)}) collective-permute-start(f32[20,16,256]{2,1,0:T(8,128)S(1)} %get-tuple-element.42), channel_id=1, source_target_pairs={{0,24},{8,16},{16,8},{24,0},{1,25},{9,17},{17,9},{25,1},{2,26},{10... | collective-permute-start | bytes 983048 | tf_op jit(solution)/shard_map/ppermute | solution.py:347
  69.9 1.3 %collective-permute-start.13 = (f32[40,128]{1,0:T(8,128)S(1)}, f32[40,128]{1,0:T(8,128)S(1)}, u32[]{:S(2)}, u32[]{:S(2)}) collective-permute-start(f32[40,128]{1,0:T(8,128)S(1)} %get-tuple-element.43), channel_id=1, source_target_pairs={{0,1},{1,0},{2,3},{3,2},{4,5},{5,4},{6,7},{7,6},{8,9},{9,8},{10,11... | collective-permute-start | bytes 61448 | tf_op jit(solution)/shard_map/ppermute | solution.py:347
  71.2 3.8 %collective-permute-start.14 = (f32[40,128]{1,0:T(8,128)S(1)}, f32[40,128]{1,0:T(8,128)S(1)}, u32[]{:S(2)}, u32[]{:S(2)}) collective-permute-start(f32[40,128]{1,0:T(8,128)S(1)} %max.18), channel_id=1, source_target_pairs={{0,2},{1,3},{2,0},{3,1},{4,6},{5,7},{6,4},{7,5},{8,10},{9,11},{10,... | collective-permute-start | bytes 61448 | tf_op jit(solution)/shard_map/ppermute | solution.py:347
  75.0 4.7 %collective-permute-start.15 = (f32[40,128]{1,0:T(8,128)S(1)}, f32[40,128]{1,0:T(8,128)S(1)}, u32[]{:S(2)}, u32[]{:S(2)}) collective-permute-start(f32[40,128]{1,0:T(8,128)S(1)} %max.19), channel_id=1, source_target_pairs={{0,4},{1,5},{2,6},{3,7},{4,0},{5,1},{6,2},{7,3},{8,12},{9,13},{10,... | collective-permute-start | bytes 61448 | tf_op jit(solution)/shard_map/ppermute | solution.py:347
  79.7 4.7 %collective-permute-start.18 = (f32[40,128]{1,0:T(8,128)S(1)}, f32[40,128]{1,0:T(8,128)S(1)}, u32[]{:S(2)}, u32[]{:S(2)}) collective-permute-start(f32[40,128]{1,0:T(8,128)S(1)} %max.20), channel_id=1, source_target_pairs={{0,24},{8,16},{16,8},{24,0},{1,25},{9,17},{17,9},{25,1},{2,26},{10... | collective-permute-start | bytes 61448 | tf_op jit(solution)/shard_map/ppermute | solution.py:347
  81.1 4.4 %collective-permute-start.17 = (f32[40,128]{1,0:T(8,128)S(1)}, f32[40,128]{1,0:T(8,128)S(1)}, u32[]{:S(2)}, u32[]{:S(2)}) collective-permute-start(f32[40,128]{1,0:T(8,128)S(1)} %max.20), channel_id=1, source_target_pairs={{0,16},{8,24},{16,0},{24,8},{1,17},{9,25},{17,1},{25,9},{2,18},{10... | collective-permute-start | bytes 61448 | tf_op jit(solution)/shard_map/ppermute | solution.py:347
  84.3 4.0 %collective-permute-start.16 = (f32[40,128]{1,0:T(8,128)S(1)}, f32[40,128]{1,0:T(8,128)S(1)}, u32[]{:S(2)}, u32[]{:S(2)}) collective-permute-start(f32[40,128]{1,0:T(8,128)S(1)} %max.20), channel_id=1, source_target_pairs={{0,8},{8,0},{16,24},{24,16},{1,9},{9,1},{17,25},{25,17},{2,10},{10... | collective-permute-start | bytes 61448 | tf_op jit(solution)/shard_map/ppermute | solution.py:347
  85.6 7.4 %collective-permute-start.7 = (f32[20,8,256]{2,1,0:T(8,128)S(1)}, f32[20,8,256]{2,1,0:T(8,128)S(1)}, u32[]{:S(2)}, u32[]{:S(2)}) collective-permute-start(f32[20,8,256]{2,1,0:T(8,128)S(1)} %get-tuple-element.36), channel_id=1, source_target_pairs={{0,8},{8,0},{16,24},{24,16},{1,9},{9,1},{17,25},{25,17},{2,10},{10... | collective-permute-start | bytes 491528 | tf_op jit(solution)/shard_map/ppermute | solution.py:347
  88.3 6.1 %collective-permute-start.8 = (f32[20,8,256]{2,1,0:T(8,128)S(1)}, f32[20,8,256]{2,1,0:T(8,128)S(1)}, u32[]{:S(2)}, u32[]{:S(2)}) collective-permute-start(f32[20,8,256]{2,1,0:T(8,128)S(1)} %get-tuple-element.37), channel_id=1, source_target_pairs={{0,16},{8,24},{16,0},{24,8},{1,17},{9,25},{17,1},{25,9},{2,18},{10... | collective-permute-start | bytes 491528 | tf_op jit(solution)/shard_map/ppermute | solution.py:347
  89.9 6.2 %collective-permute-start.9 = (f32[20,8,256]{2,1,0:T(8,128)S(1)}, f32[20,8,256]{2,1,0:T(8,128)S(1)}, u32[]{:S(2)}, u32[]{:S(2)}) collective-permute-start(f32[20,8,256]{2,1,0:T(8,128)S(1)} %get-tuple-element.38), channel_id=1, source_target_pairs={{0,24},{8,16},{16,8},{24,0},{1,25},{9,17},{17,9},{25,1},{2,26},{10... | collective-permute-start | bytes 491528 | tf_op jit(solution)/shard_map/ppermute | solution.py:347
